TPU v7x, 128 devices: a whole 4x4x4 slice. The times are simulated.
128 devices in a mesh: gx: 16 (over y, x), gy: 4 (over z), gz: 2 (over core).
Axes of the slice: x: 4, y: 4, z: 4, core: 2. Of those that a mesh axis runs over, the one named last changes fastest.
Arguments:
- load: float32 [1024, 256, 256], P('gx', 'gy', 'gz'), may hold values from -12 to 12
- stiffness: float32 [1024, 256, 256], P('gx', 'gy', 'gz'), may hold values from 0.02 to 2
- prestress: float32 [1024, 256], P(('gx', 'gy'), 'gz'), may hold values from -3 to 3
- state_var: float32 [1024, 256], P(('gx', 'gy'), 'gz'), may hold values from -1 to 1
- normal_a: float32 [1024, 256], P(('gx', 'gy'), 'gz'), may hold values from 1 to 3
Outputs:
- displacement: float32 [1024, 256, 256], P('gx', 'gy', 'gz')
- slip_rate: float32 [1024, 256], P(('gx', 'gy'), 'gz')
All inputs are finite; a program needn't handle non-finite values.
Results may differ from a plain program's by a relative error of at most 0.0003.
Values sent between devices are 32-bit elements; how exact they have to be, the bound alone decides.
A program may use at most 128 MiB of HBM per device.

v0:
```python
import functools

import jax
import jax.numpy as jnp
from jax import lax
from jax.sharding import Mesh
from jax.sharding import PartitionSpec as P

ITERS = 3
GX_GY_GZ = ("gx_0", "gx_1", "gy", "gz")
GX = ("gx_0", "gx_1")
GX_GY = ("gx_0", "gx_1", "gy")


def extended(x, sides, width):
    edges = {}
    for axis, dim in sides:
        count, length = (lax.axis_size(axis), x.shape[dim])
        up = [(i, (i + 1) % count) for i in range(count - 1)]
        last = lax.slice_in_dim(x, length - width, length, axis=dim)
        first = lax.slice_in_dim(x, 0, width, axis=dim)
        edges[dim] = (
            lax.ppermute(last, axis, up),
            lax.ppermute(first, axis, [(b, a) for a, b in up]),
        )
    done = []
    for _, dim in sides:
        low, high = edges[dim]
        around = [(width, width) if d in done else (0, 0) for d in range(x.ndim)]
        x = jnp.concatenate([jnp.pad(low, around), x, jnp.pad(high, around)], axis=dim)
        done.append(dim)
    return x


def by_axis(x, axes):
    return functools.reduce(lax.psum, axes, x)


def split_up(x, dim, count):
    lengths = x.shape
    pieces = x.reshape(*lengths[:dim], count, lengths[dim] // count, *lengths[dim + 1 :])
    return jnp.moveaxis(pieces, dim, 0)


def sum_at_owner(x, axis, dim):
    pieces = split_up(x, dim, lax.axis_size(axis))
    arrived = lax.all_to_all(pieces, axis, split_axis=0, concat_axis=0, tiled=True)
    return arrived.sum(axis=0)


def shifted(padded, sizes_now, axis_num, offset):
    slicers = [slice(2, 2 + sizes_now[0]), slice(2, 2 + sizes_now[1]), slice(2, 2 + sizes_now[2])]
    slicers[axis_num] = slice(2 + offset, 2 + offset + sizes_now[axis_num])
    return padded[tuple(slicers)]


def operate(field, stiffness):
    padded = extended(field, ((GX, 0), ("gy", 1), ("gz", 2)), 2)
    sizes_now = field.shape
    near_sum = jnp.zeros_like(field)
    for axis_num in range(3):
        near_sum = near_sum + 16.0 * (
            shifted(padded, sizes_now, axis_num, 1) + shifted(padded, sizes_now, axis_num, -1)
        )
        near_sum = near_sum - (
            shifted(padded, sizes_now, axis_num, 2) + shifted(padded, sizes_now, axis_num, -2)
        )
    return (7.5 + stiffness) * field - near_sum / 12.0


def paired_sums(residual, precond, image):
    return (
        by_axis(jnp.sum(residual * precond), GX_GY_GZ),
        by_axis(jnp.sum(image * precond), GX_GY_GZ),
    )


def per_device(load, stiffness, prestress, state_var, normal_a):
    inverse = 1.0 / (7.5 + stiffness)
    solution = jnp.zeros_like(load)
    residual = load
    precond = inverse * residual
    image = operate(precond, stiffness)
    gamma, delta = paired_sums(residual, precond, image)
    alpha = gamma / delta
    direction = precond
    along = image
    for iteration in range(ITERS):
        solution = solution + alpha * direction
        residual = residual - alpha * along
        if iteration + 1 < ITERS:
            precond = inverse * residual
            image = operate(precond, stiffness)
            gamma_new, delta = paired_sums(residual, precond, image)
            ratio = gamma_new / gamma
            alpha = gamma_new / (delta - ratio * gamma_new / alpha)
            direction = precond + ratio * direction
            along = image + ratio * along
            gamma = gamma_new
    rows_y = solution.shape[1]
    total_y = rows_y * lax.axis_size("gy")
    edge_rows = jnp.concatenate((solution[:, :2, :], solution[:, rows_y - 2 :, :]), axis=1)
    local_rows = jnp.array([0, 1, rows_y - 2, rows_y - 1], dtype=jnp.int32)
    global_y = lax.axis_index("gy") * rows_y + local_rows
    offset = global_y - (total_y // 2 - 2)
    weights = (
        (offset == 0).astype(jnp.float32)
        - 27.0 * (offset == 1).astype(jnp.float32)
        + 27.0 * (offset == 2).astype(jnp.float32)
        - (offset == 3).astype(jnp.float32)
    ) / 24.0
    fault_term = jnp.sum(edge_rows * weights[None, :, None], axis=1)
    traction = sum_at_owner(fault_term, "gy", 0)
    slip_rate = jnp.exp(-state_var) * jnp.sinh((prestress + 2.0 * traction) / normal_a)
    return (solution, slip_rate)


def solution(mesh):
    torus = Mesh(
        mesh.devices.reshape(4, 4, mesh.shape["gy"], mesh.shape["gz"]), ("gx_0", "gx_1", "gy", "gz")
    )
    in_specs = (
        P(GX, "gy", "gz"),
        P(GX, "gy", "gz"),
        P(GX_GY, "gz"),
        P(GX_GY, "gz"),
        P(GX_GY, "gz"),
    )
    out_specs = (P(GX, "gy", "gz"), P(GX_GY, "gz"))
    return jax.shard_map(
        per_device, mesh=torus, in_specs=in_specs, out_specs=out_specs, check_vma=False
    )
```

profile of v0, /device:TPU:1, one launch (start us, length us, event | category | flops | bytes accessed | tf_op | source)
XLA Modules:
  0.0 297.6 jit_solution(3604906043216781601)
XLA Ops:
  0.6 4.7 %copy_multiply_fusion = f32[64,64,128]{2,0,1:T(8,128)S(1)} fusion(f32[64,64,128]{2,1,0:T(8,128)} %param.6, f32[64,64,128]{2,1,0:T(8,128)} %param.7), kind=kLoop, calls=%fused_computation.97 | loop fusion | flops 1572864 | bytes 6291456 | tf_op jit(solution)/shard_map/mul | solution.py:82
  10.8 3.3 %collective-permute-start.4 = (f32[64,64,2]{1,0,2:T(8,128)S(1)}, f32[64,64,2]{1,0,2:T(8,128)S(1)}, u32[]{:S(2)}, u32[]{:S(2)}) collective-permute-start(f32[64,64,2]{1,0,2:T(8,128)S(1)} %copy.137), channel_id=1, source_target_pairs={{1,0},{3,2},{5,4},{7,6},{9,8},{11,10},{13,12},{15,14},{17,16},{19,... | collective-permute-start | bytes 98312 | tf_op jit(solution)/shard_map/ppermute | solution.py:24
  15.4 4.3 %collective-permute-start.3 = (f32[64,2,128]{2,0,1:T(8,128)S(1)}, f32[64,2,128]{2,0,1:T(8,128)S(1)}, u32[]{:S(2)}, u32[]{:S(2)}) collective-permute-start(f32[64,2,128]{2,0,1:T(8,128)S(1)} %get-tuple-element.72), channel_id=1, source_target_pairs={{0,2},{2,4},{4,6},{1,3},{3,5},{5,7},{8,10},{10,12},{12,14},{9,11},... | collective-permute-start | bytes 196616 | tf_op jit(solution)/shard_map/ppermute | solution.py:23
  21.0 4.0 %collective-permute-start.1 = (f32[2,64,128]{2,0,1:T(2,128)S(1)}, f32[2,64,128]{2,0,1:T(2,128)S(1)}, u32[]{:S(2)}, u32[]{:S(2)}) collective-permute-start(f32[2,64,128]{2,0,1:T(2,128)S(1)} %get-tuple-element.74), channel_id=1, source_target_pairs={{0,8},{8,16},{16,24},{24,32},{32,40},{40,48},{48,56},{56,64},{64,7... | collective-permute-start | bytes 196616 | tf_op jit(solution)/shard_map/ppermute | solution.py:23
  37.2 6.9 %select_maximum_fusion.5 = (f32[68,68,130]{2,0,1:T(8,128)}, f32[68,68,130]{2,0,1:T(8,128)}) fusion(f32[64,64,2]{2,0,1:T(8,128)S(1)} %copy-done.9, f32[68,2,128]{2,0,1:T(8,128)S(1)} %pad.38, f32[2,64,128]{2,0,1:T(2,128)S(1)} %collective-permute-done, f32[64,64,128]{2,0,1:T(8,128)S(1)} %copy_multiply_fusion, f32[2,64,128]{2,0,1:T(2,128)S(1)} %collective-permute-done.1, ...), kind=kLoop, calls=%fused_computation.6 | loop fusion | flops 8415680 | bytes 7241984 | tf_op jit(solution)/shard_map/concatenate | solution.py:30
  44.1 14.9 %multiply_reduce_fusion.3 = (f32[]{:T(128)}, f32[]{:T(128)}, f32[64,64,128]{2,0,1:T(8,128)}) fusion(f32[64,64,128]{2,0,1:T(8,128)S(1)} %copy_multiply_fusion, f32[64,64,128]{2,1,0:T(8,128)S(1)} %copy-done.5, f32[68,68,130]{2,0,1:T(8,128)} %get-tuple-element.49, f32[68,68,130]{2,0,1:T(8,128)} %get-tuple-element.48, f32[68,66,128]{2,0,1:T(8,128)S(1)} %get-tuple-element.55, ...), kind=kLoop, calls=%fused_computation.94 | loop fusion | flops 13631486 | bytes 25296904 | tf_op jit(solution)/shard_map/reduce_sum | solution.py:74
  59.0 10.6 %all-reduce.20 = (f32[]{:T(128)}, f32[]{:T(128)}) all-reduce(f32[]{:T(128)} %get-tuple-element.15, f32[]{:T(128)} %get-tuple-element.14), channel_id=1, replica_groups=mesh['gx_0'=4,'gx_1'=4,'gy'=4,'gz'=2] {'gx_0'}, use_global_device_ids=true, to_apply=%region_1.2 | all-reduce | flops 2 | bytes 16 | tf_op jit(solution)/shard_map/psum | solution.py:36
  69.5 8.7 %all-reduce.17 = (f32[]{:T(128)}, f32[]{:T(128)}) all-reduce(f32[]{:T(128)} %get-tuple-element.32, f32[]{:T(128)} %get-tuple-element.33), channel_id=1, replica_groups=mesh['gx_0'=4,'gx_1'=4,'gy'=4,'gz'=2] {'gx_1'}, use_global_device_ids=true, to_apply=%region_2.3 | all-reduce | flops 2 | bytes 16 | tf_op jit(solution)/shard_map/psum | solution.py:36
  78.2 8.3 %all-reduce.14 = (f32[]{:T(128)}, f32[]{:T(128)}) all-reduce(f32[]{:T(128)} %get-tuple-element.26, f32[]{:T(128)} %get-tuple-element.27), channel_id=1, replica_groups=mesh['gx_0'=4,'gx_1'=4,'gy'=4,'gz'=2] {'gy'}, use_global_device_ids=true, to_apply=%region_3.4 | all-reduce | flops 2 | bytes 16 | tf_op jit(solution)/shard_map/psum | solution.py:36
  86.5 10.1 %all-reduce.23 = (f32[]{:T(128)}, f32[]{:T(128)}) all-reduce(f32[]{:T(128)} %get-tuple-element.20, f32[]{:T(128)} %get-tuple-element.21), channel_id=1, replica_groups=mesh['gx_0'=4,'gx_1'=4,'gy'=4,'gz'=2] {'gz'}, use_global_device_ids=true, to_apply=%region_4.5 | all-reduce | flops 2 | bytes 16 | tf_op jit(solution)/shard_map/psum | solution.py:36
  97.9 5.3 %fusion.45 = f32[64,64,128]{2,0,1:T(8,128)S(1)} fusion(f32[64,64,128]{2,0,1:T(8,128)} %get-tuple-element.43, f32[]{:T(128)S(6)} %div.45, f32[64,64,128]{2,1,0:T(8,128)} %param.6, f32[64,64,128]{2,1,0:T(8,128)} %param.7), kind=kLoop, calls=%fused_computation.99 | loop fusion | flops 2621440 | bytes 8388612 | tf_op jit(solution)/shard_map/mul | solution.py:92
  112.3 4.0 %collective-permute-start.9 = (f32[64,2,128]{2,0,1:T(8,128)S(1)}, f32[64,2,128]{2,0,1:T(8,128)S(1)}, u32[]{:S(2)}, u32[]{:S(2)}) collective-permute-start(f32[64,2,128]{2,0,1:T(8,128)S(1)} %get-tuple-element.66), channel_id=1, source_target_pairs={{0,2},{2,4},{4,6},{1,3},{3,5},{5,7},{8,10},{10,12},{12,14},{9,11},... | collective-permute-start | bytes 196616 | tf_op jit(solution)/shard_map/ppermute | solution.py:23
  117.5 4.0 %collective-permute-start.7 = (f32[2,64,128]{2,0,1:T(2,128)S(1)}, f32[2,64,128]{2,0,1:T(2,128)S(1)}, u32[]{:S(2)}, u32[]{:S(2)}) collective-permute-start(f32[2,64,128]{2,0,1:T(2,128)S(1)} %get-tuple-element.68), channel_id=1, source_target_pairs={{0,8},{8,16},{16,24},{24,32},{32,40},{40,48},{48,56},{56,64},{64,7... | collective-permute-start | bytes 196616 | tf_op jit(solution)/shard_map/ppermute | solution.py:23
  125.7 2.9 copy.143
  134.7 6.9 %select_maximum_fusion.3 = (f32[68,68,130]{2,0,1:T(8,128)}, f32[68,68,130]{2,0,1:T(8,128)}) fusion(f32[64,64,2]{2,0,1:T(8,128)S(1)} %copy-done.10, f32[68,2,128]{2,0,1:T(8,128)S(1)} %pad.42, f32[2,64,128]{2,0,1:T(2,128)S(1)} %collective-permute-done.6, f32[64,64,128]{2,0,1:T(8,128)S(1)} %fusion.45, f32[2,64,128]{2,0,1:T(2,128)S(1)} %collective-permute-done.7, ...), kind=kLoop, calls=%fused_computation.3 | loop fusion | flops 8415680 | bytes 7241984 | tf_op jit(solution)/shard_map/concatenate | solution.py:30
  141.6 15.0 %multiply_reduce_fusion.1 = (f32[]{:T(128)}, f32[]{:T(128)}, f32[64,64,128]{2,0,1:T(8,128)}) fusion(f32[64,64,128]{2,0,1:T(8,128)S(1)} %fusion.45, f32[64,64,128]{2,0,1:T(8,128)S(1)} %copy-done.7, f32[]{:T(128)S(6)} %div.45, f32[64,64,128]{2,1,0:T(8,128)S(1)} %copy-done.6, f32[68,68,130]{2,0,1:T(8,128)} %get-tuple-element.47, ...), kind=kLoop, calls=%fused_computation.91 | loop fusion | flops 14680062 | bytes 27394060 | tf_op jit(solution)/shard_map/reduce_sum | solution.py:74
  156.6 7.5 %all-reduce.19 = (f32[]{:T(128)}, f32[]{:T(128)}) all-reduce(f32[]{:T(128)} %get-tuple-element.13, f32[]{:T(128)} %get-tuple-element.12), channel_id=1, replica_groups=mesh['gx_0'=4,'gx_1'=4,'gy'=4,'gz'=2] {'gx_0'}, use_global_device_ids=true, to_apply=%region_11.12 | all-reduce | flops 2 | bytes 16 | tf_op jit(solution)/shard_map/psum | solution.py:36
  164.2 8.3 %all-reduce.16 = (f32[]{:T(128)}, f32[]{:T(128)}) all-reduce(f32[]{:T(128)} %get-tuple-element.30, f32[]{:T(128)} %get-tuple-element.31), channel_id=1, replica_groups=mesh['gx_0'=4,'gx_1'=4,'gy'=4,'gz'=2] {'gx_1'}, use_global_device_ids=true, to_apply=%region_12.13 | all-reduce | flops 2 | bytes 16 | tf_op jit(solution)/shard_map/psum | solution.py:36
  172.4 7.5 %all-reduce.13 = (f32[]{:T(128)}, f32[]{:T(128)}) all-reduce(f32[]{:T(128)} %get-tuple-element.24, f32[]{:T(128)} %get-tuple-element.25), channel_id=1, replica_groups=mesh['gx_0'=4,'gx_1'=4,'gy'=4,'gz'=2] {'gy'}, use_global_device_ids=true, to_apply=%region_13.14 | all-reduce | flops 2 | bytes 16 | tf_op jit(solution)/shard_map/psum | solution.py:36
  179.9 10.2 %all-reduce.22 = (f32[]{:T(128)}, f32[]{:T(128)}) all-reduce(f32[]{:T(128)} %get-tuple-element.18, f32[]{:T(128)} %get-tuple-element.19), channel_id=1, replica_groups=mesh['gx_0'=4,'gx_1'=4,'gy'=4,'gz'=2] {'gz'}, use_global_device_ids=true, to_apply=%region_14.15 | all-reduce | flops 2 | bytes 16 | tf_op jit(solution)/shard_map/psum | solution.py:36
  194.6 7.3 %fusion.54 = (f32[64,64,128]{2,0,1:T(8,128)S(1)}, f32[64,64,128]{2,0,1:T(8,128)}) fusion(f32[64,64,128]{2,1,0:T(8,128)} %param.7, f32[64,64,128]{2,0,1:T(8,128)} %get-tuple-element.42, f32[64,64,128]{2,0,1:T(8,128)} %get-tuple-element.43, f32[]{:T(128)S(6)} %div.47, f32[]{:T(128)S(6)} %div.49, f32[]{:T(128)S(6)} %div.45, f32[64,64,128]{2,1,0:T(8,128)} %param.6), kind=kLoop, calls=%fused_computation.115 | loop fusion | flops 4718592 | bytes 12582924 | tf_op jit(solution)/shard_map/mul | solution.py:92
  212.3 4.0 %collective-permute-start.13 = (f32[2,64,128]{2,0,1:T(2,128)S(1)}, f32[2,64,128]{2,0,1:T(2,128)S(1)}, u32[]{:S(2)}, u32[]{:S(2)}) collective-permute-start(f32[2,64,128]{2,0,1:T(2,128)S(1)} %get-tuple-element.62), channel_id=1, source_target_pairs={{0,8},{8,16},{16,24},{24,32},{32,40},{40,48},{48,56},{56,64},{64,7... | collective-permute-start | bytes 196616 | tf_op jit(solution)/shard_map/ppermute | solution.py:23
  216.3 4.0 %collective-permute-start.15 = (f32[64,2,128]{2,0,1:T(8,128)S(1)}, f32[64,2,128]{2,0,1:T(8,128)S(1)}, u32[]{:S(2)}, u32[]{:S(2)}) collective-permute-start(f32[64,2,128]{2,0,1:T(8,128)S(1)} %get-tuple-element.60), channel_id=1, source_target_pairs={{0,2},{2,4},{4,6},{1,3},{3,5},{5,7},{8,10},{10,12},{12,14},{9,11},... | collective-permute-start | bytes 196616 | tf_op jit(solution)/shard_map/ppermute | solution.py:23
  232.4 5.8 %select_maximum_fusion.1 = (f32[68,68,130]{2,0,1:T(8,128)S(1)}, f32[68,68,130]{2,0,1:T(8,128)}) fusion(f32[64,64,2]{2,0,1:T(8,128)S(1)} %copy-done.11, f32[68,2,128]{2,0,1:T(8,128)S(1)} %pad.46, f32[2,64,128]{2,0,1:T(2,128)S(1)} %collective-permute-done.12, f32[64,64,128]{2,0,1:T(8,128)S(1)} %get-tuple-element.40, ...), kind=kLoop, calls=%fused_computation.1 | loop fusion | flops 8415680 | bytes 7241984 | tf_op jit(solution)/shard_map/concatenate | solution.py:30
  238.2 8.9 %fusion.43 = (f32[]{:T(128)}, f32[]{:T(128)}) fusion(f32[64,64,128]{2,0,1:T(8,128)S(1)} %get-tuple-element.40, f32[68,68,130]{2,0,1:T(8,128)} %get-tuple-element.45, f32[68,68,130]{2,0,1:T(8,128)S(1)} %get-tuple-element.44, f32[68,66,128]{2,0,1:T(8,128)S(1)} %get-tuple-element.51, f32[68,66,128]{2,0,1:T(8,128)S(1)} %get-tuple-element.50, ...), kind=kLoop, calls=%fused_computation.96 | loop fusion | flops 13631486 | bytes 23199752 | tf_op jit(solution)/shard_map/reduce_sum | solution.py:74
  247.1 7.5 %all-reduce.18 = (f32[]{:T(128)}, f32[]{:T(128)}) all-reduce(f32[]{:T(128)} %get-tuple-element.11, f32[]{:T(128)} %get-tuple-element.10), channel_id=1, replica_groups=mesh['gx_0'=4,'gx_1'=4,'gy'=4,'gz'=2] {'gx_0'}, use_global_device_ids=true, to_apply=%region_21.22 | all-reduce | flops 2 | bytes 16 | tf_op jit(solution)/shard_map/psum | solution.py:36
  254.6 8.6 %all-reduce.15 = (f32[]{:T(128)}, f32[]{:T(128)}) all-reduce(f32[]{:T(128)} %get-tuple-element.28, f32[]{:T(128)} %get-tuple-element.29), channel_id=1, replica_groups=mesh['gx_0'=4,'gx_1'=4,'gy'=4,'gz'=2] {'gx_1'}, use_global_device_ids=true, to_apply=%region_22.23 | all-reduce | flops 2 | bytes 16 | tf_op jit(solution)/shard_map/psum | solution.py:36
  263.2 7.2 %all-reduce.12 = (f32[]{:T(128)}, f32[]{:T(128)}) all-reduce(f32[]{:T(128)} %get-tuple-element.22, f32[]{:T(128)} %get-tuple-element.23), channel_id=1, replica_groups=mesh['gx_0'=4,'gx_1'=4,'gy'=4,'gz'=2] {'gy'}, use_global_device_ids=true, to_apply=%region_23.24 | all-reduce | flops 2 | bytes 16 | tf_op jit(solution)/shard_map/psum | solution.py:36
  270.4 9.8 %all-reduce.21 = (f32[]{:T(128)}, f32[]{:T(128)}) all-reduce(f32[]{:T(128)} %get-tuple-element.16, f32[]{:T(128)} %get-tuple-element.17), channel_id=1, replica_groups=mesh['gx_0'=4,'gx_1'=4,'gy'=4,'gz'=2] {'gz'}, use_global_device_ids=true, to_apply=%region_24.25 | all-reduce | flops 2 | bytes 16 | tf_op jit(solution)/shard_map/psum | solution.py:36
  284.2 3.0 %multiply_add_fusion = f32[64,64,128]{2,0,1:T(8,128)S(1)} fusion(f32[64,64,128]{2,0,1:T(8,128)S(1)} %get-tuple-element.40, f32[64,64,128]{2,0,1:T(8,128)} %copy-done.1, f32[64,64,128]{2,0,1:T(8,128)} %copy-done, f32[]{:T(128)S(6)} %div.51, f32[]{:T(128)S(6)} %div.53, f32[]{:T(128)S(6)} %div.47, f32[]{:T(128)S(6)} %div.49, f32[]{:T(128)S(6)} %div.45), kind=kLoop, calls=%fused_computation.88 | loop fusion | flops 4718592 | bytes 8388628 | tf_op jit(solution)/shard_map/add | solution.py:89
  289.2 3.3 %all-to-all-start = ((f32[4,16,128]{2,1,0:T(8,128)}), f32[4,16,128]{2,1,0:T(8,128)S(1)}, u32[]{:S(2)}, u32[]{:S(2)}) async-start(f32[4,16,128]{2,1,0:T(8,128)} %bitcast), calls=%async_computation | async-start | bytes 65536 | tf_op jit(solution)/shard_map/all_to_all | solution.py:47
  292.5 4.1 %copy.152 = f32[64,64,128]{2,1,0:T(8,128)} copy(f32[64,64,128]{2,0,1:T(8,128)} %copy-done.8) | data formatting | bytes 4194304
  (102 shorter events, 65.9 us)
Async XLA Ops:
  5.3 38.8 %copy-start = (f32[64,64,128]{2,0,1:T(8,128)}, f32[64,64,128]{2,0,1:T(8,128)S(1)}, u32[]{:S(2)}) copy-start(f32[64,64,128]{2,0,1:T(8,128)S(1)} %copy_multiply_fusion) | copy-start | bytes 6291460
  10.8 16.9 %collective-permute-start.4 = (f32[64,64,2]{1,0,2:T(8,128)S(1)}, f32[64,64,2]{1,0,2:T(8,128)S(1)}, u32[]{:S(2)}, u32[]{:S(2)}) collective-permute-start(f32[64,64,2]{1,0,2:T(8,128)S(1)} %copy.137), channel_id=1, source_target_pairs={{1,0},{3,2},{5,4},{7,6},{9,8},{11,10},{13,12},{15,14},{17,16},{19,... | collective-permute-start | bytes 98312 | tf_op jit(solution)/shard_map/ppermute | solution.py:24
  14.1 20.8 %collective-permute-start.2 = (f32[64,2,128]{2,0,1:T(8,128)S(1)}, f32[64,2,128]{2,0,1:T(8,128)S(1)}, u32[]{:S(2)}, u32[]{:S(2)}) collective-permute-start(f32[64,2,128]{2,0,1:T(8,128)S(1)} %get-tuple-element.73), channel_id=1, source_target_pairs={{2,0},{4,2},{6,4},{3,1},{5,3},{7,5},{10,8},{12,10},{14,12},{11,9},... | collective-permute-start | bytes 196616 | tf_op jit(solution)/shard_map/ppermute | solution.py:24
  15.4 19.6 %collective-permute-start.3 = (f32[64,2,128]{2,0,1:T(8,128)S(1)}, f32[64,2,128]{2,0,1:T(8,128)S(1)}, u32[]{:S(2)}, u32[]{:S(2)}) collective-permute-start(f32[64,2,128]{2,0,1:T(8,128)S(1)} %get-tuple-element.72), channel_id=1, source_target_pairs={{0,2},{2,4},{4,6},{1,3},{3,5},{5,7},{8,10},{10,12},{12,14},{9,11},... | collective-permute-start | bytes 196616 | tf_op jit(solution)/shard_map/ppermute | solution.py:23
  19.7 15.3 %collective-permute-start = (f32[2,64,128]{2,0,1:T(2,128)S(1)}, f32[2,64,128]{2,0,1:T(2,128)S(1)}, u32[]{:S(2)}, u32[]{:S(2)}) collective-permute-start(f32[2,64,128]{2,0,1:T(2,128)S(1)} %get-tuple-element.75), channel_id=1, source_target_pairs={{8,0},{16,8},{24,16},{32,24},{40,32},{48,40},{56,48},{64,56},{72,6... | collective-permute-start | bytes 196616 | tf_op jit(solution)/shard_map/ppermute | solution.py:24
  21.0 14.0 %collective-permute-start.1 = (f32[2,64,128]{2,0,1:T(2,128)S(1)}, f32[2,64,128]{2,0,1:T(2,128)S(1)}, u32[]{:S(2)}, u32[]{:S(2)}) collective-permute-start(f32[2,64,128]{2,0,1:T(2,128)S(1)} %get-tuple-element.74), channel_id=1, source_target_pairs={{0,8},{8,16},{16,24},{24,32},{32,40},{40,48},{48,56},{56,64},{64,7... | collective-permute-start | bytes 196616 | tf_op jit(solution)/shard_map/ppermute | solution.py:23
  27.7 4.4 %collective-permute-start.5 = (f32[64,64,2]{1,0,2:T(8,128)S(1)}, f32[64,64,2]{1,0,2:T(8,128)S(1)}, u32[]{:S(2)}, u32[]{:S(2)}) collective-permute-start(f32[64,64,2]{1,0,2:T(8,128)S(1)} %copy.139), channel_id=1, source_target_pairs={{0,1},{2,3},{4,5},{6,7},{8,9},{10,11},{12,13},{14,15},{16,17},{18,... | collective-permute-start | bytes 98312 | tf_op jit(solution)/shard_map/ppermute | solution.py:23
  37.2 6.9 %copy-start.2 = (f32[64,64,128]{2,1,0:T(8,128)S(1)}, f32[64,64,128]{2,1,0:T(8,128)}, u32[]{:S(2)}) copy-start(f32[64,64,128]{2,1,0:T(8,128)} %param.7) | copy-start | bytes 6291460
  37.2 6.9 %copy-start.5 = (f32[64,64,128]{2,1,0:T(8,128)S(1)}, f32[64,64,128]{2,1,0:T(8,128)}, u32[]{:S(2)}) copy-start(f32[64,64,128]{2,1,0:T(8,128)} %param.6) | copy-start | bytes 6291460
  103.2 38.4 %copy-start.1 = (f32[64,64,128]{2,0,1:T(8,128)}, f32[64,64,128]{2,0,1:T(8,128)S(1)}, u32[]{:S(2)}) copy-start(f32[64,64,128]{2,0,1:T(8,128)S(1)} %fusion.45) | copy-start | bytes 6291460
  108.7 15.5 %collective-permute-start.10 = (f32[64,64,2]{1,0,2:T(8,128)S(1)}, f32[64,64,2]{1,0,2:T(8,128)S(1)}, u32[]{:S(2)}, u32[]{:S(2)}) collective-permute-start(f32[64,64,2]{1,0,2:T(8,128)S(1)} %copy.142), channel_id=1, source_target_pairs={{1,0},{3,2},{5,4},{7,6},{9,8},{11,10},{13,12},{15,14},{17,16},{19,... | collective-permute-start | bytes 98312 | tf_op jit(solution)/shard_map/ppermute | solution.py:24
  111.0 20.6 %collective-permute-start.8 = (f32[64,2,128]{2,0,1:T(8,128)S(1)}, f32[64,2,128]{2,0,1:T(8,128)S(1)}, u32[]{:S(2)}, u32[]{:S(2)}) collective-permute-start(f32[64,2,128]{2,0,1:T(8,128)S(1)} %get-tuple-element.67), channel_id=1, source_target_pairs={{2,0},{4,2},{6,4},{3,1},{5,3},{7,5},{10,8},{12,10},{14,12},{11,9},... | collective-permute-start | bytes 196616 | tf_op jit(solution)/shard_map/ppermute | solution.py:24
  112.3 19.3 %collective-permute-start.9 = (f32[64,2,128]{2,0,1:T(8,128)S(1)}, f32[64,2,128]{2,0,1:T(8,128)S(1)}, u32[]{:S(2)}, u32[]{:S(2)}) collective-permute-start(f32[64,2,128]{2,0,1:T(8,128)S(1)} %get-tuple-element.66), channel_id=1, source_target_pairs={{0,2},{2,4},{4,6},{1,3},{3,5},{5,7},{8,10},{10,12},{12,14},{9,11},... | collective-permute-start | bytes 196616 | tf_op jit(solution)/shard_map/ppermute | solution.py:23
  116.2 15.3 %collective-permute-start.6 = (f32[2,64,128]{2,0,1:T(2,128)S(1)}, f32[2,64,128]{2,0,1:T(2,128)S(1)}, u32[]{:S(2)}, u32[]{:S(2)}) collective-permute-start(f32[2,64,128]{2,0,1:T(2,128)S(1)} %get-tuple-element.69), channel_id=1, source_target_pairs={{8,0},{16,8},{24,16},{32,24},{40,32},{48,40},{56,48},{64,56},{72,6... | collective-permute-start | bytes 196616 | tf_op jit(solution)/shard_map/ppermute | solution.py:24
  117.5 14.0 %collective-permute-start.7 = (f32[2,64,128]{2,0,1:T(2,128)S(1)}, f32[2,64,128]{2,0,1:T(2,128)S(1)}, u32[]{:S(2)}, u32[]{:S(2)}) collective-permute-start(f32[2,64,128]{2,0,1:T(2,128)S(1)} %get-tuple-element.68), channel_id=1, source_target_pairs={{0,8},{8,16},{16,24},{24,32},{32,40},{40,48},{48,56},{56,64},{64,7... | collective-permute-start | bytes 196616 | tf_op jit(solution)/shard_map/ppermute | solution.py:23
  124.2 4.5 %collective-permute-start.11 = (f32[64,64,2]{1,0,2:T(8,128)S(1)}, f32[64,64,2]{1,0,2:T(8,128)S(1)}, u32[]{:S(2)}, u32[]{:S(2)}) collective-permute-start(f32[64,64,2]{1,0,2:T(8,128)S(1)} %copy.144), channel_id=1, source_target_pairs={{0,1},{2,3},{4,5},{6,7},{8,9},{10,11},{12,13},{14,15},{16,17},{18,... | collective-permute-start | bytes 98312 | tf_op jit(solution)/shard_map/ppermute | solution.py:23
  131.6 3.1 %copy-start.13 = (f32[64,64,2]{2,0,1:T(8,128)S(1)}, f32[64,64,2]{2,0,1:T(8,128)}, u32[]{:S(2)}) copy-start(f32[64,64,2]{2,0,1:T(8,128)} %copy.145) | copy-start | bytes 98308
  134.7 6.9 %copy-start.3 = (f32[64,64,128]{2,1,0:T(8,128)S(1)}, f32[64,64,128]{2,1,0:T(8,128)}, u32[]{:S(2)}) copy-start(f32[64,64,128]{2,1,0:T(8,128)} %param.7) | copy-start | bytes 6291460
  134.7 6.9 %copy-start.6 = (f32[64,64,128]{2,1,0:T(8,128)S(1)}, f32[64,64,128]{2,1,0:T(8,128)}, u32[]{:S(2)}) copy-start(f32[64,64,128]{2,1,0:T(8,128)} %param.6) | copy-start | bytes 6291460
  134.7 6.9 %copy-start.7 = (f32[64,64,128]{2,0,1:T(8,128)S(1)}, f32[64,64,128]{2,0,1:T(8,128)}, u32[]{:S(2)}) copy-start(f32[64,64,128]{2,0,1:T(8,128)} %get-tuple-element.43) | copy-start | bytes 6291460
  204.7 19.6 %copy-start.18 = (s32[4]{0:T(128)S(1)}, s32[4]{0:T(128)}, u32[]{:S(2)}) copy-start(s32[4]{0:T(128)} %constant.50.clone) | copy-start | bytes 52
  207.4 15.5 %collective-permute-start.16 = (f32[64,64,2]{1,0,2:T(8,128)S(1)}, f32[64,64,2]{1,0,2:T(8,128)S(1)}, u32[]{:S(2)}, u32[]{:S(2)}) collective-permute-start(f32[64,64,2]{1,0,2:T(8,128)S(1)} %copy.146), channel_id=1, source_target_pairs={{1,0},{3,2},{5,4},{7,6},{9,8},{11,10},{13,12},{15,14},{17,16},{19,... | collective-permute-start | bytes 98312 | tf_op jit(solution)/shard_map/ppermute | solution.py:24
  209.7 20.5 %collective-permute-start.14 = (f32[64,2,128]{2,0,1:T(8,128)S(1)}, f32[64,2,128]{2,0,1:T(8,128)S(1)}, u32[]{:S(2)}, u32[]{:S(2)}) collective-permute-start(f32[64,2,128]{2,0,1:T(8,128)S(1)} %get-tuple-element.61), channel_id=1, source_target_pairs={{2,0},{4,2},{6,4},{3,1},{5,3},{7,5},{10,8},{12,10},{14,12},{11,9},... | collective-permute-start | bytes 196616 | tf_op jit(solution)/shard_map/ppermute | solution.py:24
  211.0 19.3 %collective-permute-start.12 = (f32[2,64,128]{2,0,1:T(2,128)S(1)}, f32[2,64,128]{2,0,1:T(2,128)S(1)}, u32[]{:S(2)}, u32[]{:S(2)}) collective-permute-start(f32[2,64,128]{2,0,1:T(2,128)S(1)} %get-tuple-element.63), channel_id=1, source_target_pairs={{8,0},{16,8},{24,16},{32,24},{40,32},{48,40},{56,48},{64,56},{72,6... | collective-permute-start | bytes 196616 | tf_op jit(solution)/shard_map/ppermute | solution.py:24
  212.3 18.0 %collective-permute-start.13 = (f32[2,64,128]{2,0,1:T(2,128)S(1)}, f32[2,64,128]{2,0,1:T(2,128)S(1)}, u32[]{:S(2)}, u32[]{:S(2)}) collective-permute-start(f32[2,64,128]{2,0,1:T(2,128)S(1)} %get-tuple-element.62), channel_id=1, source_target_pairs={{0,8},{8,16},{16,24},{24,32},{32,40},{40,48},{48,56},{56,64},{64,7... | collective-permute-start | bytes 196616 | tf_op jit(solution)/shard_map/ppermute | solution.py:23
  216.3 13.9 %collective-permute-start.15 = (f32[64,2,128]{2,0,1:T(8,128)S(1)}, f32[64,2,128]{2,0,1:T(8,128)S(1)}, u32[]{:S(2)}, u32[]{:S(2)}) collective-permute-start(f32[64,2,128]{2,0,1:T(8,128)S(1)} %get-tuple-element.60), channel_id=1, source_target_pairs={{0,2},{2,4},{4,6},{1,3},{3,5},{5,7},{8,10},{10,12},{12,14},{9,11},... | collective-permute-start | bytes 196616 | tf_op jit(solution)/shard_map/ppermute | solution.py:23
  222.9 4.4 %collective-permute-start.17 = (f32[64,64,2]{1,0,2:T(8,128)S(1)}, f32[64,64,2]{1,0,2:T(8,128)S(1)}, u32[]{:S(2)}, u32[]{:S(2)}) collective-permute-start(f32[64,64,2]{1,0,2:T(8,128)S(1)} %copy.148), channel_id=1, source_target_pairs={{0,1},{2,3},{4,5},{6,7},{8,9},{10,11},{12,13},{14,15},{16,17},{18,... | collective-permute-start | bytes 98312 | tf_op jit(solution)/shard_map/ppermute | solution.py:23
  232.4 5.8 %copy-start.4 = (f32[64,64,128]{2,1,0:T(8,128)S(1)}, f32[64,64,128]{2,1,0:T(8,128)}, u32[]{:S(2)}) copy-start(f32[64,64,128]{2,1,0:T(8,128)} %param.7) | copy-start | bytes 6291460
  289.2 7.5 %all-to-all-start = ((f32[4,16,128]{2,1,0:T(8,128)}), f32[4,16,128]{2,1,0:T(8,128)S(1)}, u32[]{:S(2)}, u32[]{:S(2)}) async-start(f32[4,16,128]{2,1,0:T(8,128)} %bitcast), calls=%async_computation | async-start | bytes 65536 | tf_op jit(solution)/shard_map/all_to_all | solution.py:47
  292.5 4.3 %copy-start.15 = (f32[16,128]{1,0:T(8,128)S(1)}, f32[16,128]{1,0:T(8,128)}, u32[]{:S(2)}) copy-start(f32[16,128]{1,0:T(8,128)} %param.10) | copy-start | bytes 24580
  292.5 4.3 %copy-start.16 = (f32[16,128]{1,0:T(8,128)S(1)}, f32[16,128]{1,0:T(8,128)}, u32[]{:S(2)}) copy-start(f32[16,128]{1,0:T(8,128)} %param.8) | copy-start | bytes 24580
  292.5 4.3 %copy-start.17 = (f32[16,128]{1,0:T(8,128)S(1)}, f32[16,128]{1,0:T(8,128)}, u32[]{:S(2)}) copy-start(f32[16,128]{1,0:T(8,128)} %param.9) | copy-start | bytes 24580
  (6 other events, 10.9 us)
where the time goes:
time: 304 us; the launch traced here: 298 us
  blocking collectives  104 us (34%)
  other arithmetic  82.6 us (27%)
  local copies, waits for them, and re-layouts  52.1 us (17%)
  starting transfers between devices  47.4 us (16%)
  between operations  11 us (4%)
    psum x12, blocking collectives, by_axis(): return functools.reduce(lax.psum, axes, x)  104 us
    reduce_sum x3, other arithmetic, paired_sums(): jnp.sum(image * precond)  38.8 us
    ppermute x9, starting transfers between devices, extended(): lax.ppermute(last, axis, up)  28.7 us
    concatenate x6, other arithmetic, extended(): jnp.concatenate([jnp.pad(low, around), x, jnp.pad(high, around)], axis=dim)  22.2 us
    mul x3, other arithmetic, per_device(): precond = inverse * residual  17.3 us
    slice x6, local copies, waits for them, and re-layouts, extended(): first = lax.slice_in_dim(x, 0, width, axis=dim)  16.3 us
    ppermute x9, starting transfers between devices, extended(): lax.ppermute(first, axis, [(b, a) for a, b in up])  15.5 us
    unnamed x39, local copies, waits for them, and re-layouts  10.3 us
  transfers between devices with their start and end apart: 19, of which 1 were waited for; matrix products, arithmetic and copies ran while one was open for 10% of the time, Pallas kernels for 0%

commit v1 on v0

v1 whole, which is shorter than its diff:
```python
import functools

import jax
import jax.numpy as jnp
from jax import lax
from jax.experimental import pallas as pl
from jax.experimental.pallas import tpu as pltpu
from jax.sharding import PartitionSpec as P

MESH = pl.DeviceIdType.MESH
F32 = jnp.float32
BX, BY, BZ = 64, 64, 128
LOW = 8
PITCH = BY + LOW
ROWS = (BX + 4) * PITCH + LOW
FACE = PITCH + BY
TILES = BY // 8
STRIPS = BX // 8
CHUNKS = 8


def two_sum(a, b):
    s = a + b
    t = s - a
    return s, (a - (s - t)) + (b - t)


def split(a):
    t = a * 4097.0
    high = t - (t - a)
    return high, a - high


def two_prod(a, b):
    p = a * b
    ah, al = split(a)
    bh, bl = split(b)
    return p, ((ah * bh - p) + ah * bl + al * bh) + al * bl


def norm(h, l):
    s = h + l
    return s, l - (s - h)


def dd_sub(a, b):
    s, e = two_sum(a[0], -b[0])
    return norm(s, e + (a[1] - b[1]))


def dd_mul(a, b):
    p, e = two_prod(a[0], b[0])
    return norm(p, e + (a[0] * b[1] + a[1] * b[0]))


def dd_div(a, b):
    q = a[0] / b[0]
    p, e = two_prod(q, b[0])
    r = ((a[0] - p) - e) + (a[1] - q * b[1])
    return norm(q, r / b[0])


def lane_sum(v):
    total = jnp.sum(v, axis=1, keepdims=True)
    big = total * 4096.0
    high = (v + big) - big
    low = v - high
    return norm(jnp.sum(high, axis=1, keepdims=True), jnp.sum(low, axis=1, keepdims=True))


def coefficients(mu):
    theta = dd_div(mu[1], mu[0])
    s = [None] + [dd_sub(mu[j + 1], dd_mul(theta, mu[j])) for j in range(1, 5)]
    a1 = dd_sub(dd_div(s[2], s[1]), theta)
    b1 = dd_div(s[1], mu[0])

    def second(j):
        return dd_sub(dd_sub(s[j + 1], dd_mul(a1, s[j])), dd_mul(b1, mu[j]))

    t2, t3 = second(2), second(3)
    a2 = dd_sub(dd_sub(dd_div(t3, t2), a1), theta)
    b2 = dd_div(t2, s[1])
    a0, a1, a2, b1, b2 = theta[0], a1[0], a2[0], b1[0], b2[0]
    d0 = a0
    d1 = a1 - b1 / d0
    d2 = a2 - b2 / d1
    y2 = 1.0 / (d0 * d1 * d2)
    y1 = (-1.0 / d0 - b2 * y2) / d1
    y0 = (1.0 - b1 * y1) / d0
    c2 = y2
    c1 = y1 - (a0 + a1) * y2
    c0 = y0 - a0 * y1 + (a0 * a1 - b1) * y2
    return c0, c1, c2


def spot_of(x, y=0):
    return pl.multiple_of((x + 2) * PITCH + LOW, 8) + y


def zero_edges(w):
    z8 = jnp.zeros((8, BZ), F32)
    for t in range(2 * PITCH // 8):
        w[pl.ds(8 * t, 8), :] = z8
        w[pl.ds(ROWS - LOW - 2 * PITCH + LOW + 8 * t, 8), :] = z8

    def body(x, carry):
        w[pl.ds(pl.multiple_of((x + 2) * PITCH, 8), 8), :] = z8
        return carry

    lax.fori_loop(0, BX + 1, body, 0, unroll=5)


def krylov(
    load, stiff, w0, w1, w2, coef, fault_sum,
    bv, sv, minv, ypack, zpack, trac,
    hx, hy, hz, fault, part_a, part_b,
    in_sem, xs_sem, xr_sem, ys_sem, yr_sem, zs_sem, zr_sem, fs_sem, fr_sem, rs_sem, rr_sem,
):
    gx, gy, gz = (lax.axis_index(a) for a in ("gx", "gy", "gz"))
    nx, ny, nz = (lax.axis_size(a) for a in ("gx", "gy", "gz"))
    group = ny * nz
    spot = gy * nz + gz
    lane = lax.broadcasted_iota(jnp.int32, (8, BZ), 1)
    row = lax.broadcasted_iota(jnp.int32, (8, BZ), 0)
    out_base = jnp.where(gz == 0, BZ - 2, 0)
    in_base = jnp.where(gz == 0, 0, BZ - 2)
    out_lane = lane - out_base
    in_mask = ((lane - in_base) & (BZ - 1)) < 2

    step = BX // CHUNKS
    loads = []
    for i in range(CHUNKS):
        part = pl.ds(i * step, step)
        a = pltpu.make_async_copy(load.at[part], bv.at[part], in_sem.at[0, i])
        b = pltpu.make_async_copy(stiff.at[part], sv.at[part], in_sem.at[1, i])
        a.start()
        b.start()
        loads.append((a, b))

    barrier = pltpu.get_barrier_semaphore()
    peers = []
    for r in range(1, group):
        other = lax.rem(spot + r, group)
        peers.append((gx, other // nz, lax.rem(other, nz)))
    cross = [(lax.rem(gx + r, nx), gy, gz) for r in range(1, nx)]
    for peer in peers + cross:
        pl.semaphore_signal(barrier, inc=1, device_id=peer, device_id_type=MESH)

    for w in (w0, w1, w2):
        zero_edges(w)

    zero = jnp.zeros((8, BZ), F32)
    mu0 = zero
    for i in range(CHUNKS):
        loads[i][0].wait()
        loads[i][1].wait()

        def start_plane(x, acc):
            for t in range(TILES):
                at = pl.ds(8 * t, 8)
                b = bv[x, at, :]
                inverse = 1.0 / (7.5 + sv[x, at, :])
                w = b * inverse
                w0[pl.ds(spot_of(x, 8 * t), 8), :] = w
                minv[pl.ds(pl.multiple_of(x * BY, 8) + 8 * t, 8), :] = inverse * (1.0 / 12.0)
                acc = acc + b * w
            return acc

        mu0 = mu0 + lax.fori_loop(i * step, (i + 1) * step, start_plane, zero)

    pl.semaphore_wait(barrier, len(peers) + len(cross))

    def remote(src, dst, send, recv, device):
        return pltpu.make_async_remote_copy(
            src_ref=src, dst_ref=dst, send_sem=send, recv_sem=recv,
            device_id=device, device_id_type=MESH,
        )

    def x_copy(w, k, side):
        plane = 0 if side == 0 else BX - 2
        return remote(
            w.at[pl.ds(spot_of(plane), FACE), :], hx.at[k, 1 - side],
            xs_sem.at[k, side], xr_sem.at[k, 1 - side],
            (gx - 1 if side == 0 else gx + 1, gy, gz),
        )

    def y_copy(k, side):
        return remote(
            ypack.at[k, side], hy.at[k, 1 - side],
            ys_sem.at[k, side], yr_sem.at[k, 1 - side],
            (gx, gy - 1 if side == 0 else gy + 1, gz),
        )

    def z_copy(k):
        return remote(zpack.at[k], hz.at[k], zs_sem.at[k], zr_sem.at[k], (gx, gy, 1 - gz))

    has_x = (gx > 0, gx < nx - 1)
    has_y = (gy > 0, gy < ny - 1)
    near_fault = (gy == ny // 2 - 1) | (gy == ny // 2)
    source = gy - (ny // 2 - 1)
    low_side = jnp.where(gy == ny // 2, 1.0, 0.0)
    high_side = jnp.where(gy == ny // 2 - 1, 1.0, 0.0)
    own_rows = BX // ny

    def fault_copy(k, r):
        owner = lax.rem(gy + r, ny)
        return remote(
            trac.at[k, pl.ds(owner * own_rows, own_rows), :], fault.at[source, k],
            fs_sem.at[k, r - 1], fr_sem.at[source, k], (gx, owner, gz),
        )

    def exchange(w, k):
        for j in range(STRIPS):
            strip = []
            for n, y in enumerate((0, 1, BY - 2, BY - 1)):
                v = w[pl.ds(spot_of(8 * j, y), 8, stride=PITCH), :]
                ypack[k, n // 2, n % 2, pl.ds(8 * j, 8), :] = v
                strip.append(v)
            term = low_side * (27.0 * strip[0] - strip[1]) + high_side * (strip[2] - 27.0 * strip[3])
            trac[k, pl.ds(8 * j, 8), :] = term / 24.0
        for side in range(2):
            @pl.when(has_x[side])
            def _(side=side):
                x_copy(w, k, side).start()
        for side in range(2):
            @pl.when(has_y[side])
            def _(side=side):
                y_copy(k, side).start()

        def pack(x, acc):
            mask = ((out_lane - 2 * x) & (BZ - 1)) < 2
            return tuple(
                jnp.where(mask, pltpu.roll(w[pl.ds(spot_of(x, 8 * t), 8), :], 2 * x, 1), acc[t])
                for t in range(TILES)
            )

        packed = lax.fori_loop(0, BX, pack, (zero,) * TILES)
        for t in range(TILES):
            zpack[k, t] = packed[t]

        @pl.when(near_fault)
        def _():
            for r in range(1, ny):
                fault_copy(k, r).start()
            for i in range(own_rows // 8):
                fault[source, k, pl.ds(8 * i, 8), :] = trac[
                    k, pl.ds(pl.multiple_of(gy * own_rows + 8 * i, 8), 8), :
                ]

        z_copy(k).start()

    def bulk(w, out, k, init):
        z_copy(k).wait_recv()

        def plane(x, acc):
            for t in range(TILES):
                def at(dx, dy):
                    return w[pl.ds(spot_of(x, 8 * t) + (dx * PITCH + dy), 8), :]

                c = at(0, 0)
                h = pltpu.roll(hz[k, t], lax.rem(BZ - 2 * x, BZ), 1)
                h = jnp.where(in_mask, h, 0.0)
                r1 = pltpu.roll(jnp.where(lane == 0, h, c), BZ - 1, 1)
                r2 = pltpu.roll(jnp.where(lane < 2, h, c), BZ - 2, 1)
                l1 = pltpu.roll(jnp.where(lane == BZ - 1, h, c), 1, 1)
                l2 = pltpu.roll(jnp.where(lane >= BZ - 2, h, c), 2, 1)
                near = (at(1, 0) + at(-1, 0)) + (r1 + l1) + (at(0, 1) + at(0, -1))
                far = (at(2, 0) + at(-2, 0)) + (r2 + l2) + (at(0, 2) + at(0, -2))
                n = 16.0 * near - far
                acc = out(x, t, c, n, acc)
            return acc

        return lax.fori_loop(0, BX, plane, init)

    def fixes(k, apply_x, apply_y):
        for side in range(2):
            @pl.when(has_x[side])
            def _(side=side):
                x_copy(w0, k, 1 - side).wait_recv()
                inner, outer = (1, 0) if side == 0 else (0, 1)
                first, second = (0, 1) if side == 0 else (BX - 1, BX - 2)
                for t in range(TILES):
                    close = hx[k, side, pl.ds(inner * PITCH + 8 * t, 8), :]
                    distant = hx[k, side, pl.ds(outer * PITCH + 8 * t, 8), :]
                    apply_x(first, t, 16.0 * close - distant)
                    apply_x(second, t, -close)
        for side in range(2):
            @pl.when(has_y[side])
            def _(side=side):
                y_copy(k, 1 - side).wait_recv()
                inner, outer = (1, 0) if side == 0 else (0, 1)
                first, second = (0, 1) if side == 0 else (BY - 1, BY - 2)
                for j in range(STRIPS):
                    at = pl.ds(8 * j, 8)
                    close = hy[k, side, inner, at, :]
                    apply_y(j, first, 16.0 * close - hy[k, side, outer, at, :])
                    apply_y(j, second, -close)

    def basis_step(w, new, k, moments, init):
        exchange(w, k)

        def out(x, t, c, n, acc):
            new[pl.ds(spot_of(x, 8 * t), 8), :] = (
                c - minv[pl.ds(pl.multiple_of(x * BY, 8) + 8 * t, 8), :] * n
            )
            return moments(x, t, c, acc)

        sums = bulk(w, out, k, init)

        def apply_x(x, t, n):
            at = pl.ds(spot_of(x, 8 * t), 8)
            new[at, :] = new[at, :] - minv[pl.ds(x * BY + 8 * t, 8), :] * n

        def apply_y(j, y, n):
            at = pl.ds(spot_of(8 * j, y), 8, stride=PITCH)
            new[at, :] = new[at, :] - minv[pl.ds(8 * j * BY + y, 8, stride=BY), :] * n

        fixes(k, apply_x, apply_y)
        return sums

    basis_step(w0, w1, 0, lambda x, t, c, acc: acc, 0)

    def first_moments(x, t, c, acc):
        at = pl.ds(8 * t, 8)
        return (acc[0] + bv[x, at, :] * c, acc[1] + ((7.5 + sv[x, at, :]) * c) * c)

    mu1, mu2 = basis_step(w1, w2, 1, first_moments, (zero, zero))

    exchange(w2, 2)

    def last(x, t, c, n, acc):
        d = (7.5 + sv[x, pl.ds(8 * t, 8), :]) * c
        return (
            acc[0] + d * w1[pl.ds(spot_of(x, 8 * t), 8), :],
            acc[1] + d * c,
            acc[2] + c * (d - n * (1.0 / 12.0)),
        )

    mu3, mu4, mu5 = bulk(w2, last, 2, (zero, zero, zero))
    part_a[0] = zero

    def cross_x(x, t, n):
        part_a[0] = part_a[0] + w2[pl.ds(spot_of(x, 8 * t), 8), :] * n

    def cross_y(j, y, n):
        part_a[0] = part_a[0] + w2[pl.ds(spot_of(8 * j, y), 8, stride=PITCH), :] * n

    fixes(2, cross_x, cross_y)
    mu5 = mu5 - part_a[0] * (1.0 / 12.0)

    local = zero
    for j, m in enumerate((mu0, mu1, mu2, mu3, mu4, mu5)):
        local = jnp.where(row == j, jnp.sum(m, axis=0, keepdims=True), local)

    def reduce(value, buf, s, devices):
        buf[0] = value
        copies = [
            remote(buf.at[0], buf.at[r + 1], rs_sem.at[s, r], rr_sem.at[s, r], device)
            for r, device in enumerate(devices)
        ]
        for c in copies:
            c.start()
        for c in copies:
            c.wait_recv()
        total = value
        for r in range(len(devices)):
            total = total + buf[r + 1]
        return total, copies

    total, sent_a = reduce(local, part_a, 0, peers)
    total, sent_b = reduce(total, part_b, 1, cross)

    mu = []
    for j in range(6):
        mu.append(lane_sum(jnp.broadcast_to(total[j : j + 1, :], (8, BZ))))
    for j, c in enumerate(coefficients(mu)):
        coef[j] = jnp.broadcast_to(c, (8, BZ))

    for k in range(3):
        for s in range(2):
            @pl.when(gy != ny // 2 - 1 + s)
            def _(k=k, s=s):
                remote(
                    trac.at[k, pl.ds(0, own_rows), :], fault.at[s, k],
                    fs_sem.at[k, 0], fr_sem.at[s, k], (gx, gy, 1 - gz),
                ).wait_recv()
    for k in range(3):
        for i in range(own_rows // 8):
            at = pl.ds(8 * i, 8)
            fault_sum[k, at, :] = fault[0, k, at, :] + fault[1, k, at, :]

    for c in sent_a + sent_b:
        c.wait_send()
    for k in range(3):
        for side in range(2):
            @pl.when(has_x[side])
            def _(k=k, side=side):
                x_copy(w0, k, side).wait_send()
            @pl.when(has_y[side])
            def _(k=k, side=side):
                y_copy(k, side).wait_send()
        z_copy(k).wait_send()

        @pl.when(near_fault)
        def _(k=k):
            for r in range(1, ny):
                fault_copy(k, r).wait_send()


def combine(w0, w1, w2, coef, fault_sum, prestress, state, normal, u, slip, buf, sem):
    c0, c1, c2 = coef[0], coef[1], coef[2]
    step = BX // CHUNKS
    copies = []
    for i in range(CHUNKS):
        def plane(x, carry):
            for t in range(TILES):
                at = pl.ds(spot_of(x, 8 * t), 8)
                buf[x, pl.ds(8 * t, 8), :] = (c0 * w0[at, :] + c1 * w1[at, :]) + c2 * w2[at, :]
            return carry

        lax.fori_loop(i * step, (i + 1) * step, plane, 0)
        part = pl.ds(i * step, step)
        copy = pltpu.make_async_copy(buf.at[part], u.at[part], sem.at[i])
        copy.start()
        copies.append(copy)
    for i in range(slip.shape[0] // 8):
        at = pl.ds(8 * i, 8)
        traction = (c0 * fault_sum[0, at, :] + c1 * fault_sum[1, at, :]) + c2 * fault_sum[2, at, :]
        x = (prestress[at, :] + 2.0 * traction) / normal[at, :]
        half = 0.6931471805599453
        large = jnp.exp(x - half) - jnp.exp(-x - half)
        q = x * x
        small = x * (1.0 + q * (1 / 6 + q * (1 / 120 + q * (1 / 5040 + q * (1 / 362880 + q / 39916800)))))
        sinh = jnp.where(jnp.abs(x) < 1.0, small, large)
        slip[at, :] = jnp.exp(-state[at, :]) * sinh
    for copy in copies:
        copy.wait()


def per_device(load, stiffness, prestress, state_var, normal_a):
    vmem = pl.BlockSpec(memory_space=pltpu.VMEM)
    hbm = pl.BlockSpec(memory_space=pl.ANY)
    ny = lax.axis_size("gy")
    own = BX // ny
    group = ny * lax.axis_size("gz")
    nx = lax.axis_size("gx")
    big = (ROWS, BZ)
    DMA = pltpu.SemaphoreType.DMA
    outs = pl.pallas_call(
        krylov,
        out_shape=[
            pltpu.VMEM(big, F32), pltpu.VMEM(big, F32), pltpu.VMEM(big, F32),
            pltpu.VMEM((3, 8, BZ), F32), pltpu.VMEM((3, own, BZ), F32),
        ],
        in_specs=[pl.BlockSpec(memory_space=pltpu.HBM)] * 2,
        out_specs=[vmem] * 5,
        scratch_shapes=[
            pltpu.VMEM((BX, BY, BZ), F32),
            pltpu.VMEM((BX, BY, BZ), F32),
            pltpu.VMEM((BX * BY, BZ), F32),
            pltpu.VMEM((3, 2, 2, BX, BZ), F32),
            pltpu.VMEM((3, TILES, 8, BZ), F32),
            pltpu.VMEM((3, BX, BZ), F32),
            pltpu.VMEM((3, 2, FACE, BZ), F32),
            pltpu.VMEM((3, 2, 2, BX, BZ), F32),
            pltpu.VMEM((3, TILES, 8, BZ), F32),
            pltpu.VMEM((2, 3, own, BZ), F32),
            pltpu.VMEM((group, 8, BZ), F32),
            pltpu.VMEM((nx, 8, BZ), F32),
            DMA((2, CHUNKS)),
            DMA((3, 2)), DMA((3, 2)), DMA((3, 2)), DMA((3, 2)), DMA((3,)), DMA((3,)),
            DMA((3, ny - 1)), DMA((2, 3)),
            DMA((2, nx - 1)), DMA((2, nx - 1)),
        ],
        compiler_params=pltpu.CompilerParams(
            collective_id=0, has_side_effects=True, vmem_limit_bytes=40 * 2**20
        ),
        name="krylov",
    )(load, stiffness)
    return pl.pallas_call(
        combine,
        out_shape=[
            jax.ShapeDtypeStruct(load.shape, F32),
            jax.ShapeDtypeStruct(prestress.shape, F32),
        ],
        in_specs=[vmem] * 8,
        out_specs=[hbm, vmem],
        scratch_shapes=[pltpu.VMEM((BX, BY, BZ), F32), DMA((CHUNKS,))],
        compiler_params=pltpu.CompilerParams(vmem_limit_bytes=24 * 2**20),
        name="combine",
    )(*outs, prestress, state_var, normal_a)


def solution(mesh):
    block = P("gx", "gy", "gz")
    fault = P(("gx", "gy"), "gz")
    return jax.shard_map(
        per_device,
        mesh=mesh,
        in_specs=(block, block, fault, fault, fault),
        out_specs=(block, fault),
        check_vma=False,
    )
```

time: 304 us -> 75.7 us (0.25); the launches traced: 298 us -> 75.6 us
  blocking collectives: 104 us -> 0 us
  other arithmetic: 82.6 us -> 0 us
  Pallas kernels: 0 us -> 71.7 us
  local copies, waits for them, and re-layouts: 52.1 us -> 3.19 us
  starting transfers between devices: 47.4 us -> 0 us
  between operations: 11 us -> 0.67 us
    psum x12 -> x0, blocking collectives: 104 us -> none  [by_axis(): return functools.reduce(lax.psum, axes, x)]
    pallas_call x0 -> x2, Pallas kernels: none -> 71.7 us  [the longest x1 69.6 us: per_device(): pl.pallas_call(krylov, out_shape=[pltpu.VMEM(big, F32), pltpu.VMEM(big, F...]
    ppermute x18 -> x0, starting transfers between devices: 44.2 us -> none  [the longest x9 28.7 us: extended(): lax.ppermute(last, axis, up)]
    reduce_sum x5 -> x0, other arithmetic: 39.5 us -> none  [the longest x3 38.8 us: paired_sums(): jnp.sum(image * precond)]
    slice x16 -> x0, local copies, waits for them, and re-layouts: 24.4 us -> none  [the longest x6 16.3 us: extended(): first = lax.slice_in_dim(x, 0, width, axis=dim)]
    concatenate x6 -> x0, other arithmetic: 22.2 us -> none  [extended(): jnp.concatenate([jnp.pad(low, around), x, jnp.pad(high, around)], axis=dim)]
    mul x4 -> x0, other arithmetic: 17.9 us -> none  [the longest x3 17.3 us: per_device(): precond = inverse * residual]
    ppermute x6 -> x0, local copies, waits for them, and re-layouts: 17.4 us -> none  [the longest x3 8.69 us: extended(): lax.ppermute(first, axis, [(b, a) for a, b in up])]
  transfers between devices with their start and end apart: 19 -> 0, of which waited for: 1 -> 0; matrix products, arithmetic and copies ran while one was open for 10% -> 0% of each run, Pallas kernels for 0% -> 0%
where the time goes in v1:
time: 75.7 us; the launch traced here: 75.6 us
  Pallas kernels  71.7 us (95%)
  local copies, waits for them, and re-layouts  3.19 us (4%)
    pallas_call x1, Pallas kernels, per_device(): pl.pallas_call(krylov, out_shape=[pltpu.VMEM(big, F32), pltpu.VMEM(big, F...  69.6 us
    unnamed x10, local copies, waits for them, and re-layouts  3.19 us
    pallas_call x1, Pallas kernels, per_device(): pl.pallas_call(combine, out_shape=[jax.ShapeDtypeStruct(load.shape, F32),...  2.09 us

profile of v1, /device:TPU:1, one launch (start us, length us, event | category | flops | bytes accessed | tf_op | source)
XLA Modules:
  0.0 75.6 jit_solution(16499549060126632235)
XLA Ops:
  0.6 0.0 copy-start
  0.6 1.6 %copy-done = f32[64,64,128]{2,1,0:T(8,128)S(1)} copy-done((f32[64,64,128]{2,1,0:T(8,128)S(1)}, f32[64,64,128]{2,1,0:T(8,128)}, u32[]{:S(2)}) %copy-start) | copy-done | bytes 2097176
  2.2 0.0 copy-start.1
  2.2 1.6 %copy-done.1 = f32[64,64,128]{2,1,0:T(8,128)S(1)} copy-done((f32[64,64,128]{2,1,0:T(8,128)S(1)}, f32[64,64,128]{2,1,0:T(8,128)}, u32[]{:S(2)}) %copy-start.1) | copy-done | bytes 2097176
  3.8 0.0 copy-start.2
  3.8 0.0 copy-start.3
  3.8 0.0 copy-start.4
  3.8 69.6 %krylov.1 = (f32[4904,128]{1,0:T(8,128)S(1)}, f32[4904,128]{1,0:T(8,128)S(1)}, f32[4904,128]{1,0:T(8,128)S(1)}, f32[3,8,128]{2,1,0:T(8,128)S(1)}, f32[3,16,128]{2,1,0:T(8,128)S(1)}) custom-call(f32[64,64,128]{2,1,0:T(8,128)S(1)} %copy-done, f32[64,64,128]{2,1,0:T(8,128)S(1)} %copy-done.1), custom_call_target="tpu_custom_call" | custom-call | tf_op jit(solution)/shard_map/krylov/pallas_call | solution.py:449
  73.4 0.0 copy-done.2
  73.4 0.0 copy-done.3
  73.5 0.0 copy-done.4
  73.5 2.1 %combine.1 = (f32[64,64,128]{2,1,0:T(8,128)}, f32[16,128]{1,0:T(8,128)}) custom-call(f32[4904,128]{1,0:T(8,128)S(1)} %get-tuple-element.7.w0, f32[4904,128]{1,0:T(8,128)S(1)} %get-tuple-element.8.w1, f32[4904,128]{1,0:T(8,128)S(1)} %get-tuple-element.9.w2, f32[3,8,128]{2,1,0:T(8,128)S(1)} %get-tuple-element.10.coef, ...), custom_call_target="tpu_custom_call" | custom-call | tf_op jit(solution)/shard_map/combine/pallas_call | solution.py:480
Async XLA Ops:
  0.6 1.6 %copy-start = (f32[64,64,128]{2,1,0:T(8,128)S(1)}, f32[64,64,128]{2,1,0:T(8,128)}, u32[]{:S(2)}) copy-start(f32[64,64,128]{2,1,0:T(8,128)} %load.1) | copy-start | bytes 6291460
  2.2 1.6 %copy-start.1 = (f32[64,64,128]{2,1,0:T(8,128)S(1)}, f32[64,64,128]{2,1,0:T(8,128)}, u32[]{:S(2)}) copy-start(f32[64,64,128]{2,1,0:T(8,128)} %stiff.1) | copy-start | bytes 6291460
  3.8 69.6 %copy-start.2 = (f32[16,128]{1,0:T(8,128)S(1)}, f32[16,128]{1,0:T(8,128)}, u32[]{:S(2)}) copy-start(f32[16,128]{1,0:T(8,128)} %prestress.1) | copy-start | bytes 24580
  3.8 69.6 %copy-start.3 = (f32[16,128]{1,0:T(8,128)S(1)}, f32[16,128]{1,0:T(8,128)}, u32[]{:S(2)}) copy-start(f32[16,128]{1,0:T(8,128)} %state.1) | copy-start | bytes 24580
  3.8 69.6 %copy-start.4 = (f32[16,128]{1,0:T(8,128)S(1)}, f32[16,128]{1,0:T(8,128)}, u32[]{:S(2)}) copy-start(f32[16,128]{1,0:T(8,128)} %normal.1) | copy-start | bytes 24580

commit v2 on v1

--- a/solution.py
+++ b/solution.py
@@ -17,6 +17,8 @@
 TILES = BY // 8
 STRIPS = BX // 8
 CHUNKS = 8
+SLOTS = 32
+UNROLL = 8
 
 
 def two_sum(a, b):
@@ -112,7 +114,7 @@
 
 def krylov(
     load, stiff, w0, w1, w2, coef, fault_sum,
-    bv, sv, minv, ypack, zpack, trac,
+    bv, sv, minv, ypack, zpack, edge, trac,
     hx, hy, hz, fault, part_a, part_b,
     in_sem, xs_sem, xr_sem, ys_sem, yr_sem, zs_sem, zr_sem, fs_sem, fr_sem, rs_sem, rr_sem,
 ):
@@ -122,10 +124,9 @@
     spot = gy * nz + gz
     lane = lax.broadcasted_iota(jnp.int32, (8, BZ), 1)
     row = lax.broadcasted_iota(jnp.int32, (8, BZ), 0)
-    out_base = jnp.where(gz == 0, BZ - 2, 0)
-    in_base = jnp.where(gz == 0, 0, BZ - 2)
-    out_lane = lane - out_base
-    in_mask = ((lane - in_base) & (BZ - 1)) < 2
+    place = (lane + 2) & 3
+    halo_here = (place >> 1) == (1 - gz)
+    packs = (BX // SLOTS) * TILES
 
     step = BX // CHUNKS
     loads = []
@@ -166,7 +167,7 @@
                 acc = acc + b * w
             return acc
 
-        mu0 = mu0 + lax.fori_loop(i * step, (i + 1) * step, start_plane, zero)
+        mu0 = lax.fori_loop(i * step, (i + 1) * step, start_plane, mu0, unroll=min(step, UNROLL))
 
     pl.semaphore_wait(barrier, len(peers) + len(cross))
 
@@ -227,16 +228,21 @@
             def _(side=side):
                 y_copy(k, side).start()
 
-        def pack(x, acc):
-            mask = ((out_lane - 2 * x) & (BZ - 1)) < 2
-            return tuple(
-                jnp.where(mask, pltpu.roll(w[pl.ds(spot_of(x, 8 * t), 8), :], 2 * x, 1), acc[t])
-                for t in range(TILES)
-            )
-
-        packed = lax.fori_loop(0, BX, pack, (zero,) * TILES)
-        for t in range(TILES):
-            zpack[k, t] = packed[t]
+        for half in range(BX // SLOTS):
+            def pack(q, acc, half=half):
+                mask = ((lane + 2 - 4 * q) & (BZ - 1)) < 4
+                return tuple(
+                    jnp.where(
+                        mask,
+                        pltpu.roll(w[pl.ds(spot_of(half * SLOTS + q, 8 * t), 8), :], 4 * q, 1),
+                        acc[t],
+                    )
+                    for t in range(TILES)
+                )
+
+            packed = lax.fori_loop(0, SLOTS, pack, (zero,) * TILES, unroll=2 * UNROLL)
+            for t in range(TILES):
+                zpack[k, half * TILES + t] = packed[t]
 
         @pl.when(near_fault)
         def _():
@@ -249,28 +255,38 @@
 
         z_copy(k).start()
 
-    def bulk(w, out, k, init):
-        z_copy(k).wait_recv()
+    def edge_terms(d):
+        near = jnp.where(place == 1, pltpu.roll(d, BZ - 1, 1), pltpu.roll(d, 1, 1))
+        near = jnp.where((place == 1) | (place == 2), near, 0.0)
+        return 16.0 * near - jnp.where(place < 2, pltpu.roll(d, BZ - 2, 1), pltpu.roll(d, 2, 1))
+
+    def bulk(w, out, k, init, with_halo):
+        if with_halo:
+            z_copy(k).wait_recv()
+        for i in range(packs):
+            d = -zpack[k, i]
+            if with_halo:
+                d = d + jnp.where(halo_here, hz[k, i], 0.0)
+            edge[i] = edge_terms(d)
 
         def plane(x, acc):
+            q = lax.rem(x, SLOTS)
+            mask = ((lane + 2) & (BZ - 1)) < 4
             for t in range(TILES):
                 def at(dx, dy):
                     return w[pl.ds(spot_of(x, 8 * t) + (dx * PITCH + dy), 8), :]
 
                 c = at(0, 0)
-                h = pltpu.roll(hz[k, t], lax.rem(BZ - 2 * x, BZ), 1)
-                h = jnp.where(in_mask, h, 0.0)
-                r1 = pltpu.roll(jnp.where(lane == 0, h, c), BZ - 1, 1)
-                r2 = pltpu.roll(jnp.where(lane < 2, h, c), BZ - 2, 1)
-                l1 = pltpu.roll(jnp.where(lane == BZ - 1, h, c), 1, 1)
-                l2 = pltpu.roll(jnp.where(lane >= BZ - 2, h, c), 2, 1)
-                near = (at(1, 0) + at(-1, 0)) + (r1 + l1) + (at(0, 1) + at(0, -1))
-                far = (at(2, 0) + at(-2, 0)) + (r2 + l2) + (at(0, 2) + at(0, -2))
-                n = 16.0 * near - far
+                e = pltpu.roll(edge[(x // SLOTS) * TILES + t], lax.rem(BZ - 4 * q, BZ), 1)
+                near = pltpu.roll(c, BZ - 1, 1) + pltpu.roll(c, 1, 1)
+                far = pltpu.roll(c, BZ - 2, 1) + pltpu.roll(c, 2, 1)
+                near = (at(1, 0) + at(-1, 0)) + near + (at(0, 1) + at(0, -1))
+                far = (at(2, 0) + at(-2, 0)) + far + (at(0, 2) + at(0, -2))
+                n = (16.0 * near - far) + jnp.where(mask, e, 0.0)
                 acc = out(x, t, c, n, acc)
             return acc
 
-        return lax.fori_loop(0, BX, plane, init)
+        return lax.fori_loop(0, BX, plane, init, unroll=UNROLL)
 
     def fixes(k, apply_x, apply_y):
         for side in range(2):
@@ -305,7 +321,7 @@
             )
             return moments(x, t, c, acc)
 
-        sums = bulk(w, out, k, init)
+        sums = bulk(w, out, k, init, True)
 
         def apply_x(x, t, n):
             at = pl.ds(spot_of(x, 8 * t), 8)
@@ -336,7 +352,7 @@
             acc[2] + c * (d - n * (1.0 / 12.0)),
         )
 
-    mu3, mu4, mu5 = bulk(w2, last, 2, (zero, zero, zero))
+    mu3, mu4, mu5 = bulk(w2, last, 2, (zero, zero, zero), False)
     part_a[0] = zero
 
     def cross_x(x, t, n):
@@ -345,8 +361,12 @@
     def cross_y(j, y, n):
         part_a[0] = part_a[0] + w2[pl.ds(spot_of(8 * j, y), 8, stride=PITCH), :] * n
 
+    z_copy(2).wait_recv()
+    crossing = zero
+    for i in range(packs):
+        crossing = crossing + zpack[2, i] * edge_terms(jnp.where(halo_here, hz[2, i], 0.0))
     fixes(2, cross_x, cross_y)
-    mu5 = mu5 - part_a[0] * (1.0 / 12.0)
+    mu5 = mu5 - (part_a[0] + crossing) * (1.0 / 12.0)
 
     local = zero
     for j, m in enumerate((mu0, mu1, mu2, mu3, mu4, mu5)):
@@ -445,6 +465,7 @@
     group = ny * lax.axis_size("gz")
     nx = lax.axis_size("gx")
     big = (ROWS, BZ)
+    packs = (BX // SLOTS) * TILES
     DMA = pltpu.SemaphoreType.DMA
     outs = pl.pallas_call(
         krylov,
@@ -459,11 +480,12 @@
             pltpu.VMEM((BX, BY, BZ), F32),
             pltpu.VMEM((BX * BY, BZ), F32),
             pltpu.VMEM((3, 2, 2, BX, BZ), F32),
-            pltpu.VMEM((3, TILES, 8, BZ), F32),
+            pltpu.VMEM((3, packs, 8, BZ), F32),
+            pltpu.VMEM((packs, 8, BZ), F32),
             pltpu.VMEM((3, BX, BZ), F32),
             pltpu.VMEM((3, 2, FACE, BZ), F32),
             pltpu.VMEM((3, 2, 2, BX, BZ), F32),
-            pltpu.VMEM((3, TILES, 8, BZ), F32),
+            pltpu.VMEM((3, packs, 8, BZ), F32),
             pltpu.VMEM((2, 3, own, BZ), F32),
             pltpu.VMEM((group, 8, BZ), F32),
             pltpu.VMEM((nx, 8, BZ), F32),
@@ -473,7 +495,7 @@
             DMA((2, nx - 1)), DMA((2, nx - 1)),
         ],
         compiler_params=pltpu.CompilerParams(
-            collective_id=0, has_side_effects=True, vmem_limit_bytes=40 * 2**20
+            collective_id=0, has_side_effects=True, vmem_limit_bytes=55 * 2**20
         ),
         name="krylov",
     )(load, stiffness)

time: 75.7 us -> 36.5 us (0.48)
  Pallas kernels: 71.7 us -> 35.7 us
  local copies, waits for them, and re-layouts: 3.19 us -> 0.01 us
    pallas_call x1, Pallas kernels: 69.6 us -> 33.6 us  [per_device(): pl.pallas_call(krylov, out_shape=[pltpu.VMEM(big, F32), pltpu.VMEM(big, F...]
    unnamed x10 -> x6, local copies, waits for them, and re-layouts: 3.19 us -> 0.01 us
where the time goes in v2:
time: 36.5 us; the launch traced here: 36.4 us
  Pallas kernels  35.7 us (98%)
  between operations  0.69 us (2%)
    pallas_call x1, Pallas kernels, per_device(): pl.pallas_call(krylov, out_shape=[pltpu.VMEM(big, F32), pltpu.VMEM(big, F...  33.6 us
    pallas_call x1, Pallas kernels, per_device(): pl.pallas_call(combine, out_shape=[jax.ShapeDtypeStruct(load.shape, F32),...  2.09 us

profile of v2, /device:TPU:1, one launch (start us, length us, event | category | flops | bytes accessed | tf_op | source)
XLA Modules:
  0.0 36.4 jit_solution(7481896735828905735)
XLA Ops:
  0.6 0.0 copy-start.2
  0.6 0.0 copy-start.1
  0.7 0.0 copy-start
  0.7 33.6 %krylov.1 = (f32[4904,128]{1,0:T(8,128)S(1)}, f32[4904,128]{1,0:T(8,128)S(1)}, f32[4904,128]{1,0:T(8,128)S(1)}, f32[3,8,128]{2,1,0:T(8,128)S(1)}, f32[3,16,128]{2,1,0:T(8,128)S(1)}) custom-call(f32[64,64,128]{2,1,0:T(8,128)} %load.1, f32[64,64,128]{2,1,0:T(8,128)} %stiff.1), custom_call_target="tpu_custom_call" | custom-call | tf_op jit(solution)/shard_map/krylov/pallas_call | solution.py:470
  34.3 0.0 copy-done.2
  34.3 0.0 copy-done.1
  34.3 0.0 copy-done
  34.3 2.1 %combine.1 = (f32[64,64,128]{2,1,0:T(8,128)}, f32[16,128]{1,0:T(8,128)}) custom-call(f32[4904,128]{1,0:T(8,128)S(1)} %get-tuple-element.7.w0, f32[4904,128]{1,0:T(8,128)S(1)} %get-tuple-element.8.w1, f32[4904,128]{1,0:T(8,128)S(1)} %get-tuple-element.9.w2, f32[3,8,128]{2,1,0:T(8,128)S(1)} %get-tuple-element.10.coef, ...), custom_call_target="tpu_custom_call" | custom-call | tf_op jit(solution)/shard_map/combine/pallas_call | solution.py:502
Async XLA Ops:
  0.6 33.7 %copy-start.2 = (f32[16,128]{1,0:T(8,128)S(1)}, f32[16,128]{1,0:T(8,128)}, u32[]{:S(2)}) copy-start(f32[16,128]{1,0:T(8,128)} %normal.1) | copy-start | bytes 24580
  0.6 33.7 %copy-start.1 = (f32[16,128]{1,0:T(8,128)S(1)}, f32[16,128]{1,0:T(8,128)}, u32[]{:S(2)}) copy-start(f32[16,128]{1,0:T(8,128)} %state.1) | copy-start | bytes 24580
  0.7 33.7 %copy-start = (f32[16,128]{1,0:T(8,128)S(1)}, f32[16,128]{1,0:T(8,128)}, u32[]{:S(2)}) copy-start(f32[16,128]{1,0:T(8,128)} %prestress.1) | copy-start | bytes 24580

commit v3 on v2

--- a/solution.py
+++ b/solution.py
@@ -116,7 +116,7 @@
     load, stiff, w0, w1, w2, coef, fault_sum,
     bv, sv, minv, ypack, zpack, edge, trac,
     hx, hy, hz, fault, part_a, part_b,
-    in_sem, xs_sem, xr_sem, ys_sem, yr_sem, zs_sem, zr_sem, fs_sem, fr_sem, rs_sem, rr_sem,
+    in_sem, xs_sem, xr_sem, ys_sem, yr_sem, zs_sem, zr_sem, fs_sem, fr_sem, rs_sem, rr_sem, token,
 ):
     gx, gy, gz = (lax.axis_index(a) for a in ("gx", "gy", "gz"))
     nx, ny, nz = (lax.axis_size(a) for a in ("gx", "gy", "gz"))
@@ -130,7 +130,8 @@
 
     step = BX // CHUNKS
     loads = []
-    for i in range(CHUNKS):
+    order = [0, CHUNKS - 1] + list(range(1, CHUNKS - 1))
+    for i in order:
         part = pl.ds(i * step, step)
         a = pltpu.make_async_copy(load.at[part], bv.at[part], in_sem.at[0, i])
         b = pltpu.make_async_copy(stiff.at[part], sv.at[part], in_sem.at[1, i])
@@ -144,32 +145,43 @@
         other = lax.rem(spot + r, group)
         peers.append((gx, other // nz, lax.rem(other, nz)))
     cross = [(lax.rem(gx + r, nx), gy, gz) for r in range(1, nx)]
-    for peer in peers + cross:
-        pl.semaphore_signal(barrier, inc=1, device_id=peer, device_id_type=MESH)
+    has_x = (gx > 0, gx < nx - 1)
+    has_y = (gy > 0, gy < ny - 1)
+
+    def one(flag):
+        return jnp.where(flag, 1, 0)
+
+    def sides(distance):
+        return ((gx >= distance, gx - distance), (gx + distance < nx, gx + distance))
+
+    def signal(k, distance):
+        for side, (there, target) in enumerate(sides(distance)):
+            @pl.when(there)
+            def _(side=side, target=target):
+                pl.semaphore_signal(
+                    token.at[k, 1 - side], inc=1, device_id=(target, gy, gz), device_id_type=MESH
+                )
+
+    def await_signals(k, distance):
+        for side, (there, _) in enumerate(sides(distance)):
+            @pl.when(there)
+            def _(side=side):
+                pl.semaphore_wait(token.at[k, side], 1)
+
+    for there, target in sides(1):
+        @pl.when(there)
+        def _(target=target):
+            pl.semaphore_signal(barrier, inc=1, device_id=(target, gy, gz), device_id_type=MESH)
+    for side in range(2):
+        @pl.when(has_y[side])
+        def _(side=side):
+            pl.semaphore_signal(
+                barrier, inc=1, device_id=(gx, gy + 2 * side - 1, gz), device_id_type=MESH
+            )
+    pl.semaphore_signal(barrier, inc=1, device_id=(gx, gy, 1 - gz), device_id_type=MESH)
 
     for w in (w0, w1, w2):
         zero_edges(w)
-
-    zero = jnp.zeros((8, BZ), F32)
-    mu0 = zero
-    for i in range(CHUNKS):
-        loads[i][0].wait()
-        loads[i][1].wait()
-
-        def start_plane(x, acc):
-            for t in range(TILES):
-                at = pl.ds(8 * t, 8)
-                b = bv[x, at, :]
-                inverse = 1.0 / (7.5 + sv[x, at, :])
-                w = b * inverse
-                w0[pl.ds(spot_of(x, 8 * t), 8), :] = w
-                minv[pl.ds(pl.multiple_of(x * BY, 8) + 8 * t, 8), :] = inverse * (1.0 / 12.0)
-                acc = acc + b * w
-            return acc
-
-        mu0 = lax.fori_loop(i * step, (i + 1) * step, start_plane, mu0, unroll=min(step, UNROLL))
-
-    pl.semaphore_wait(barrier, len(peers) + len(cross))
 
     def remote(src, dst, send, recv, device):
         return pltpu.make_async_remote_copy(
@@ -177,17 +189,30 @@
             device_id=device, device_id_type=MESH,
         )
 
-    def x_copy(w, k, side):
+    def x_copies(w, k, side):
         plane = 0 if side == 0 else BX - 2
+        device = (gx - 1 if side == 0 else gx + 1, gy, gz)
+        if k < 2:
+            return [
+                remote(
+                    w.at[pl.ds(spot_of(plane), FACE), :], hx.at[k, 1 - side],
+                    xs_sem.at[k, side, 0], xr_sem.at[k, 1 - side, 0], device,
+                )
+            ]
+        half = BY // 2
+        return [
+            remote(
+                w.at[pl.ds(spot_of(plane + n, side * half), half), :],
+                hx.at[k, 1 - side, pl.ds(n * PITCH + side * half, half), :],
+                xs_sem.at[k, side, n], xr_sem.at[k, 1 - side, n], device,
+            )
+            for n in range(2)
+        ]
+
+    def y_copy(k, side):
+        strips = pl.ds(0, BX) if k < 2 else pl.ds(side * (BX // 2), BX // 2)
         return remote(
-            w.at[pl.ds(spot_of(plane), FACE), :], hx.at[k, 1 - side],
-            xs_sem.at[k, side], xr_sem.at[k, 1 - side],
-            (gx - 1 if side == 0 else gx + 1, gy, gz),
-        )
-
-    def y_copy(k, side):
-        return remote(
-            ypack.at[k, side], hy.at[k, 1 - side],
+            ypack.at[k, side, :, strips, :], hy.at[k, 1 - side, :, strips, :],
             ys_sem.at[k, side], yr_sem.at[k, 1 - side],
             (gx, gy - 1 if side == 0 else gy + 1, gz),
         )
@@ -195,8 +220,6 @@
     def z_copy(k):
         return remote(zpack.at[k], hz.at[k], zs_sem.at[k], zr_sem.at[k], (gx, gy, 1 - gz))
 
-    has_x = (gx > 0, gx < nx - 1)
-    has_y = (gy > 0, gy < ny - 1)
     near_fault = (gy == ny // 2 - 1) | (gy == ny // 2)
     source = gy - (ny // 2 - 1)
     low_side = jnp.where(gy == ny // 2, 1.0, 0.0)
@@ -209,6 +232,23 @@
             trac.at[k, pl.ds(owner * own_rows, own_rows), :], fault.at[source, k],
             fs_sem.at[k, r - 1], fr_sem.at[source, k], (gx, owner, gz),
         )
+
+    def send_x(w, k):
+        for side in range(2):
+            @pl.when(has_x[side])
+            def _(side=side):
+                for copy in x_copies(w, k, side):
+                    copy.start()
+
+    def send_fault(k):
+        @pl.when(near_fault)
+        def _():
+            for r in range(1, ny):
+                fault_copy(k, r).start()
+            for i in range(own_rows // 8):
+                fault[source, k, pl.ds(8 * i, 8), :] = trac[
+                    k, pl.ds(pl.multiple_of(gy * own_rows + 8 * i, 8), 8), :
+                ]
 
     def exchange(w, k):
         for j in range(STRIPS):
@@ -219,10 +259,6 @@
                 strip.append(v)
             term = low_side * (27.0 * strip[0] - strip[1]) + high_side * (strip[2] - 27.0 * strip[3])
             trac[k, pl.ds(8 * j, 8), :] = term / 24.0
-        for side in range(2):
-            @pl.when(has_x[side])
-            def _(side=side):
-                x_copy(w, k, side).start()
         for side in range(2):
             @pl.when(has_y[side])
             def _(side=side):
@@ -244,16 +280,36 @@
             for t in range(TILES):
                 zpack[k, half * TILES + t] = packed[t]
 
-        @pl.when(near_fault)
-        def _():
-            for r in range(1, ny):
-                fault_copy(k, r).start()
-            for i in range(own_rows // 8):
-                fault[source, k, pl.ds(8 * i, 8), :] = trac[
-                    k, pl.ds(pl.multiple_of(gy * own_rows + 8 * i, 8), 8), :
-                ]
-
         z_copy(k).start()
+        if k == 2:
+            for n in range(3):
+                send_fault(n)
+
+    zero = jnp.zeros((8, BZ), F32)
+    mu0 = zero
+    for n, i in enumerate(order):
+        first_wait, second_wait = loads[n]
+        first_wait.wait()
+        second_wait.wait()
+
+        def start_plane(x, acc):
+            for t in range(TILES):
+                at = pl.ds(8 * t, 8)
+                b = bv[x, at, :]
+                inverse = 1.0 / (7.5 + sv[x, at, :])
+                w = b * inverse
+                w0[pl.ds(spot_of(x, 8 * t), 8), :] = w
+                minv[pl.ds(pl.multiple_of(x * BY, 8) + 8 * t, 8), :] = inverse * (1.0 / 12.0)
+                acc = acc + b * w
+            return acc
+
+        mu0 = lax.fori_loop(i * step, (i + 1) * step, start_plane, mu0, unroll=min(step, UNROLL))
+        if n == 1:
+            pl.semaphore_wait(
+                barrier,
+                1 + one(has_x[0]) + one(has_x[1]) + one(has_y[0]) + one(has_y[1]),
+            )
+            send_x(w0, 0)
 
     def edge_terms(d):
         near = jnp.where(place == 1, pltpu.roll(d, BZ - 1, 1), pltpu.roll(d, 1, 1))
@@ -289,28 +345,36 @@
         return lax.fori_loop(0, BX, plane, init, unroll=UNROLL)
 
     def fixes(k, apply_x, apply_y):
-        for side in range(2):
-            @pl.when(has_x[side])
-            def _(side=side):
-                x_copy(w0, k, 1 - side).wait_recv()
-                inner, outer = (1, 0) if side == 0 else (0, 1)
-                first, second = (0, 1) if side == 0 else (BX - 1, BX - 2)
-                for t in range(TILES):
-                    close = hx[k, side, pl.ds(inner * PITCH + 8 * t, 8), :]
-                    distant = hx[k, side, pl.ds(outer * PITCH + 8 * t, 8), :]
-                    apply_x(first, t, 16.0 * close - distant)
-                    apply_x(second, t, -close)
+        whole = k < 2
         for side in range(2):
             @pl.when(has_y[side])
             def _(side=side):
                 y_copy(k, 1 - side).wait_recv()
                 inner, outer = (1, 0) if side == 0 else (0, 1)
                 first, second = (0, 1) if side == 0 else (BY - 1, BY - 2)
-                for j in range(STRIPS):
+                span = range(STRIPS)
+                if not whole:
+                    span = range((1 - side) * STRIPS // 2, (2 - side) * STRIPS // 2)
+                for j in span:
                     at = pl.ds(8 * j, 8)
                     close = hy[k, side, inner, at, :]
                     apply_y(j, first, 16.0 * close - hy[k, side, outer, at, :])
                     apply_y(j, second, -close)
+        for side in range(2):
+            @pl.when(has_x[side])
+            def _(side=side):
+                for copy in x_copies(w0, k, 1 - side):
+                    copy.wait_recv()
+                inner, outer = (1, 0) if side == 0 else (0, 1)
+                first, second = (0, 1) if side == 0 else (BX - 1, BX - 2)
+                span = range(TILES)
+                if not whole:
+                    span = range((1 - side) * TILES // 2, (2 - side) * TILES // 2)
+                for t in span:
+                    close = hx[k, side, pl.ds(inner * PITCH + 8 * t, 8), :]
+                    distant = hx[k, side, pl.ds(outer * PITCH + 8 * t, 8), :]
+                    apply_x(first, t, 16.0 * close - distant)
+                    apply_x(second, t, -close)
 
     def basis_step(w, new, k, moments, init):
         exchange(w, k)
@@ -332,6 +396,10 @@
             new[at, :] = new[at, :] - minv[pl.ds(8 * j * BY + y, 8, stride=BY), :] * n
 
         fixes(k, apply_x, apply_y)
+        if k > 0:
+            await_signals(k - 1, 1 << k)
+        send_x(new, k + 1)
+        signal(k, 2 << k)
         return sums
 
     basis_step(w0, w1, 0, lambda x, t, c, acc: acc, 0)
@@ -366,7 +434,9 @@
     for i in range(packs):
         crossing = crossing + zpack[2, i] * edge_terms(jnp.where(halo_here, hz[2, i], 0.0))
     fixes(2, cross_x, cross_y)
-    mu5 = mu5 - (part_a[0] + crossing) * (1.0 / 12.0)
+    mu5 = mu5 - (2.0 * part_a[0] + crossing) * (1.0 / 12.0)
+    await_signals(1, 4)
+    signal(2, 8)
 
     local = zero
     for j, m in enumerate((mu0, mu1, mu2, mu3, mu4, mu5)):
@@ -388,6 +458,7 @@
         return total, copies
 
     total, sent_a = reduce(local, part_a, 0, peers)
+    await_signals(2, 8)
     total, sent_b = reduce(total, part_b, 1, cross)
 
     mu = []
@@ -415,7 +486,8 @@
         for side in range(2):
             @pl.when(has_x[side])
             def _(k=k, side=side):
-                x_copy(w0, k, side).wait_send()
+                for copy in x_copies(w0, k, side):
+                    copy.wait_send()
             @pl.when(has_y[side])
             def _(k=k, side=side):
                 y_copy(k, side).wait_send()
@@ -490,9 +562,10 @@
             pltpu.VMEM((group, 8, BZ), F32),
             pltpu.VMEM((nx, 8, BZ), F32),
             DMA((2, CHUNKS)),
-            DMA((3, 2)), DMA((3, 2)), DMA((3, 2)), DMA((3, 2)), DMA((3,)), DMA((3,)),
+            DMA((3, 2, 2)), DMA((3, 2, 2)), DMA((3, 2)), DMA((3, 2)), DMA((3,)), DMA((3,)),
             DMA((3, ny - 1)), DMA((2, 3)),
             DMA((2, nx - 1)), DMA((2, nx - 1)),
+            pltpu.SemaphoreType.REGULAR((3, 2)),
         ],
         compiler_params=pltpu.CompilerParams(
             collective_id=0, has_side_effects=True, vmem_limit_bytes=55 * 2**20

time: 36.5 us -> 36.6 us (level)
  no operation moved by 1% of the time
where the time goes in v3:
time: 36.6 us; the launch traced here: 36.5 us
  Pallas kernels  35.8 us (98%)
  between operations  0.69 us (2%)
    pallas_call x1, Pallas kernels, per_device(): pl.pallas_call(krylov, out_shape=[pltpu.VMEM(big, F32), pltpu.VMEM(big, F...  33.7 us
    pallas_call x1, Pallas kernels, per_device(): pl.pallas_call(combine, out_shape=[jax.ShapeDtypeStruct(load.shape, F32),...  2.09 us

profile of v3, /device:TPU:1, one launch (start us, length us, event | category | flops | bytes accessed | tf_op | source)
XLA Modules:
  0.0 36.5 jit_solution(14417689863216240742)
XLA Ops:
  0.6 0.0 copy-start.2
  0.6 0.0 copy-start.1
  0.7 0.0 copy-start
  0.7 33.7 %krylov.1 = (f32[4904,128]{1,0:T(8,128)S(1)}, f32[4904,128]{1,0:T(8,128)S(1)}, f32[4904,128]{1,0:T(8,128)S(1)}, f32[3,8,128]{2,1,0:T(8,128)S(1)}, f32[3,16,128]{2,1,0:T(8,128)S(1)}) custom-call(f32[64,64,128]{2,1,0:T(8,128)} %load.1, f32[64,64,128]{2,1,0:T(8,128)} %stiff.1), custom_call_target="tpu_custom_call" | custom-call | tf_op jit(solution)/shard_map/krylov/pallas_call | solution.py:542
  34.4 0.0 copy-done.2
  34.4 0.0 copy-done.1
  34.4 0.0 copy-done
  34.4 2.1 %combine.1 = (f32[64,64,128]{2,1,0:T(8,128)}, f32[16,128]{1,0:T(8,128)}) custom-call(f32[4904,128]{1,0:T(8,128)S(1)} %get-tuple-element.7.w0, f32[4904,128]{1,0:T(8,128)S(1)} %get-tuple-element.8.w1, f32[4904,128]{1,0:T(8,128)S(1)} %get-tuple-element.9.w2, f32[3,8,128]{2,1,0:T(8,128)S(1)} %get-tuple-element.10.coef, ...), custom_call_target="tpu_custom_call" | custom-call | tf_op jit(solution)/shard_map/combine/pallas_call | solution.py:575
Async XLA Ops:
  0.6 33.8 %copy-start.2 = (f32[16,128]{1,0:T(8,128)S(1)}, f32[16,128]{1,0:T(8,128)}, u32[]{:S(2)}) copy-start(f32[16,128]{1,0:T(8,128)} %normal.1) | copy-start | bytes 24580
  0.6 33.8 %copy-start.1 = (f32[16,128]{1,0:T(8,128)S(1)}, f32[16,128]{1,0:T(8,128)}, u32[]{:S(2)}) copy-start(f32[16,128]{1,0:T(8,128)} %state.1) | copy-start | bytes 24580
  0.7 33.8 %copy-start = (f32[16,128]{1,0:T(8,128)S(1)}, f32[16,128]{1,0:T(8,128)}, u32[]{:S(2)}) copy-start(f32[16,128]{1,0:T(8,128)} %prestress.1) | copy-start | bytes 24580

commit v4 on v3

--- a/solution.py
+++ b/solution.py
@@ -9,6 +9,7 @@
 
 MESH = pl.DeviceIdType.MESH
 F32 = jnp.float32
+BF16 = jnp.bfloat16
 BX, BY, BZ = 64, 64, 128
 LOW = 8
 PITCH = BY + LOW
@@ -18,6 +19,7 @@
 STRIPS = BX // 8
 CHUNKS = 8
 SLOTS = 32
+GROUP = 4
 UNROLL = 8
 
 
@@ -115,7 +117,7 @@
 def krylov(
     load, stiff, w0, w1, w2, coef, fault_sum,
     bv, sv, minv, ypack, zpack, edge, trac,
-    hx, hy, hz, fault, part_a, part_b,
+    hx, hy, hz, fault, part_a, part_b, band, even, odd,
     in_sem, xs_sem, xr_sem, ys_sem, yr_sem, zs_sem, zr_sem, fs_sem, fr_sem, rs_sem, rr_sem, token,
 ):
     gx, gy, gz = (lax.axis_index(a) for a in ("gx", "gy", "gz"))
@@ -285,6 +287,10 @@
             for n in range(3):
                 send_fault(n)
 
+    at_row = lax.rem(lax.broadcasted_iota(jnp.int32, (3 * BZ, BZ), 0), BZ)
+    gap = jnp.abs(at_row - lax.broadcasted_iota(jnp.int32, (3 * BZ, BZ), 1))
+    band[...] = jnp.where(gap == 1, 16.0, jnp.where(gap == 2, -1.0, 0.0)).astype(BF16)
+
     zero = jnp.zeros((8, BZ), F32)
     mu0 = zero
     for n, i in enumerate(order):
@@ -316,33 +322,51 @@
         near = jnp.where((place == 1) | (place == 2), near, 0.0)
         return 16.0 * near - jnp.where(place < 2, pltpu.roll(d, BZ - 2, 1), pltpu.roll(d, 2, 1))
 
+    def along_z(w, x):
+        c = w[pl.ds(spot_of(x), GROUP * PITCH), :]
+        high = c.astype(BF16)
+        rest = c - high.astype(F32)
+        middle = rest.astype(BF16)
+        low = (rest - middle.astype(F32)).astype(BF16)
+        return jnp.dot(
+            jnp.concatenate([high, middle, low], axis=1), band[...], preferred_element_type=F32
+        )
+
     def bulk(w, out, k, init, with_halo):
         if with_halo:
             z_copy(k).wait_recv()
-        for i in range(packs):
-            d = -zpack[k, i]
-            if with_halo:
-                d = d + jnp.where(halo_here, hz[k, i], 0.0)
-            edge[i] = edge_terms(d)
-
-        def plane(x, acc):
-            q = lax.rem(x, SLOTS)
-            mask = ((lane + 2) & (BZ - 1)) < 4
+            for i in range(packs):
+                edge[i] = edge_terms(jnp.where(halo_here, hz[k, i], 0.0))
+        mask = ((lane + 2) & (BZ - 1)) < 4
+
+        def group(g, zz, acc):
             for t in range(TILES):
-                def at(dx, dy):
-                    return w[pl.ds(spot_of(x, 8 * t) + (dx * PITCH + dy), 8), :]
-
-                c = at(0, 0)
-                e = pltpu.roll(edge[(x // SLOTS) * TILES + t], lax.rem(BZ - 4 * q, BZ), 1)
-                near = pltpu.roll(c, BZ - 1, 1) + pltpu.roll(c, 1, 1)
-                far = pltpu.roll(c, BZ - 2, 1) + pltpu.roll(c, 2, 1)
-                near = (at(1, 0) + at(-1, 0)) + near + (at(0, 1) + at(0, -1))
-                far = (at(2, 0) + at(-2, 0)) + far + (at(0, 2) + at(0, -2))
-                n = (16.0 * near - far) + jnp.where(mask, e, 0.0)
-                acc = out(x, t, c, n, acc)
+                def at(p, dy):
+                    return w[pl.ds(spot_of(g * GROUP, 8 * t) + (p * PITCH + dy), 8), :]
+
+                line = [at(p, 0) for p in range(-2, GROUP + 2)]
+                for p in range(GROUP):
+                    x = g * GROUP + p
+                    near = (line[p + 3] + line[p + 1]) + (at(p, 1) + at(p, -1))
+                    far = (line[p + 4] + line[p]) + (at(p, 2) + at(p, -2))
+                    n = (16.0 * near - far) + zz[pl.ds(p * PITCH + 8 * t, 8), :]
+                    if with_halo:
+                        turn = lax.rem(BZ - 4 * lax.rem(x, SLOTS), BZ)
+                        e = pltpu.roll(edge[(x // SLOTS) * TILES + t], turn, 1)
+                        n = n + jnp.where(mask, e, 0.0)
+                    acc = out(x, t, line[p + 2], n, acc)
             return acc
 
-        return lax.fori_loop(0, BX, plane, init, unroll=UNROLL)
+        groups = BX // GROUP
+        even[...] = along_z(w, 0)
+
+        def pair(i, acc):
+            odd[...] = along_z(w, (2 * i + 1) * GROUP)
+            acc = group(2 * i, even, acc)
+            even[...] = along_z(w, jnp.minimum(2 * i + 2, groups - 1) * GROUP)
+            return group(2 * i + 1, odd, acc)
+
+        return lax.fori_loop(0, groups // 2, pair, init)
 
     def fixes(k, apply_x, apply_y):
         whole = k < 2
@@ -561,6 +585,9 @@
             pltpu.VMEM((2, 3, own, BZ), F32),
             pltpu.VMEM((group, 8, BZ), F32),
             pltpu.VMEM((nx, 8, BZ), F32),
+            pltpu.VMEM((3 * BZ, BZ), BF16),
+            pltpu.VMEM((GROUP * PITCH, BZ), F32),
+            pltpu.VMEM((GROUP * PITCH, BZ), F32),
             DMA((2, CHUNKS)),
             DMA((3, 2, 2)), DMA((3, 2, 2)), DMA((3, 2)), DMA((3, 2)), DMA((3,)), DMA((3,)),
             DMA((3, ny - 1)), DMA((2, 3)),

time: 36.6 us -> 34.1 us (0.932)
  Pallas kernels: 35.8 us -> 33.3 us
    pallas_call x1, Pallas kernels: 33.7 us -> 31.2 us  [per_device(): pl.pallas_call(krylov, out_shape=[pltpu.VMEM(big, F32), pltpu.VMEM(big, F...]
where the time goes in v4:
time: 34.1 us; the launch traced here: 34 us
  Pallas kernels  33.3 us (98%)
  between operations  0.69 us (2%)
    pallas_call x1, Pallas kernels, per_device(): pl.pallas_call(krylov, out_shape=[pltpu.VMEM(big, F32), pltpu.VMEM(big, F...  31.2 us
    pallas_call x1, Pallas kernels, per_device(): pl.pallas_call(combine, out_shape=[jax.ShapeDtypeStruct(load.shape, F32),...  2.09 us

profile of v4, /device:TPU:1, one launch (start us, length us, event | category | flops | bytes accessed | tf_op | source)
XLA Modules:
  0.0 34.0 jit_solution(13268391478575695720)
XLA Ops:
  0.6 0.0 copy-start.2
  0.6 0.0 copy-start.1
  0.7 0.0 copy-start
  0.7 31.2 %krylov.1 = (f32[4904,128]{1,0:T(8,128)S(1)}, f32[4904,128]{1,0:T(8,128)S(1)}, f32[4904,128]{1,0:T(8,128)S(1)}, f32[3,8,128]{2,1,0:T(8,128)S(1)}, f32[3,16,128]{2,1,0:T(8,128)S(1)}) custom-call(f32[64,64,128]{2,1,0:T(8,128)} %load.1, f32[64,64,128]{2,1,0:T(8,128)} %stiff.1), custom_call_target="tpu_custom_call" | custom-call | tf_op jit(solution)/shard_map/krylov/pallas_call | solution.py:566
  31.9 0.0 copy-done.2
  31.9 0.0 copy-done.1
  31.9 0.0 copy-done
  31.9 2.1 %combine.1 = (f32[64,64,128]{2,1,0:T(8,128)}, f32[16,128]{1,0:T(8,128)}) custom-call(f32[4904,128]{1,0:T(8,128)S(1)} %get-tuple-element.7.w0, f32[4904,128]{1,0:T(8,128)S(1)} %get-tuple-element.8.w1, f32[4904,128]{1,0:T(8,128)S(1)} %get-tuple-element.9.w2, f32[3,8,128]{2,1,0:T(8,128)S(1)} %get-tuple-element.10.coef, ...), custom_call_target="tpu_custom_call" | custom-call | tf_op jit(solution)/shard_map/combine/pallas_call | solution.py:602
Async XLA Ops:
  0.6 31.3 %copy-start.2 = (f32[16,128]{1,0:T(8,128)S(1)}, f32[16,128]{1,0:T(8,128)}, u32[]{:S(2)}) copy-start(f32[16,128]{1,0:T(8,128)} %normal.1) | copy-start | bytes 24580
  0.6 31.3 %copy-start.1 = (f32[16,128]{1,0:T(8,128)S(1)}, f32[16,128]{1,0:T(8,128)}, u32[]{:S(2)}) copy-start(f32[16,128]{1,0:T(8,128)} %state.1) | copy-start | bytes 24580
  0.7 31.3 %copy-start = (f32[16,128]{1,0:T(8,128)S(1)}, f32[16,128]{1,0:T(8,128)}, u32[]{:S(2)}) copy-start(f32[16,128]{1,0:T(8,128)} %prestress.1) | copy-start | bytes 24580

commit v5 on v4

--- a/solution.py
+++ b/solution.py
@@ -14,10 +14,10 @@
 LOW = 8
 PITCH = BY + LOW
 ROWS = (BX + 4) * PITCH + LOW
-FACE = PITCH + BY
 TILES = BY // 8
 STRIPS = BX // 8
 CHUNKS = 8
+INNER = 6
 SLOTS = 32
 GROUP = 4
 UNROLL = 8
@@ -62,14 +62,6 @@
     p, e = two_prod(q, b[0])
     r = ((a[0] - p) - e) + (a[1] - q * b[1])
     return norm(q, r / b[0])
-
-
-def lane_sum(v):
-    total = jnp.sum(v, axis=1, keepdims=True)
-    big = total * 4096.0
-    high = (v + big) - big
-    low = v - high
-    return norm(jnp.sum(high, axis=1, keepdims=True), jnp.sum(low, axis=1, keepdims=True))
 
 
 def coefficients(mu):
@@ -116,8 +108,8 @@
 
 def krylov(
     load, stiff, w0, w1, w2, coef, fault_sum,
-    bv, sv, minv, ypack, zpack, edge, trac,
-    hx, hy, hz, fault, part_a, part_b, band, even, odd,
+    bs, minv, ypack, zpack, edge, trac,
+    hx, hy, hz, fault, part_a, part_b, cross_sum, band, even, odd,
     in_sem, xs_sem, xr_sem, ys_sem, yr_sem, zs_sem, zr_sem, fs_sem, fr_sem, rs_sem, rr_sem, token,
 ):
     gx, gy, gz = (lax.axis_index(a) for a in ("gx", "gy", "gz"))
@@ -129,17 +121,17 @@
     place = (lane + 2) & 3
     halo_here = (place >> 1) == (1 - gz)
     packs = (BX // SLOTS) * TILES
-
-    step = BX // CHUNKS
-    loads = []
-    order = [0, CHUNKS - 1] + list(range(1, CHUNKS - 1))
-    for i in order:
-        part = pl.ds(i * step, step)
-        a = pltpu.make_async_copy(load.at[part], bv.at[part], in_sem.at[0, i])
-        b = pltpu.make_async_copy(stiff.at[part], sv.at[part], in_sem.at[1, i])
-        a.start()
-        b.start()
-        loads.append((a, b))
+    zero = jnp.zeros((8, BZ), F32)
+
+    regions = [
+        (0, 2, 0, BY), (BX - 2, BX, 0, BY), (2, BX - 2, 0, 8), (2, BX - 2, BY - 8, BY)
+    ]
+    cuts = [2 + (BX - 4) * i // INNER for i in range(INNER + 1)]
+    regions += [(lo, hi, 8, BY - 8) for lo, hi in zip(cuts, cuts[1:])]
+    for n, (xa, xb, ya, yb) in enumerate(regions):
+        part = (pl.ds(xa, xb - xa), pl.ds(ya, yb - ya))
+        for i, source in enumerate((load, stiff)):
+            pltpu.make_async_copy(source.at[part], bs.at[(i,) + part], in_sem.at[n]).start()
 
     barrier = pltpu.get_barrier_semaphore()
     peers = []
@@ -185,31 +177,34 @@
     for w in (w0, w1, w2):
         zero_edges(w)
 
+    at_row = lax.rem(lax.broadcasted_iota(jnp.int32, (3 * BZ, BZ), 0), BZ)
+    gap = jnp.abs(at_row - lax.broadcasted_iota(jnp.int32, (3 * BZ, BZ), 1))
+    band[...] = jnp.where(gap == 1, 16.0, jnp.where(gap == 2, -1.0, 0.0)).astype(BF16)
+
     def remote(src, dst, send, recv, device):
         return pltpu.make_async_remote_copy(
             src_ref=src, dst_ref=dst, send_sem=send, recv_sem=recv,
             device_id=device, device_id_type=MESH,
         )
 
-    def x_copies(w, k, side):
-        plane = 0 if side == 0 else BX - 2
+    partner = (gx, gy, 1 - gz)
+    half = BY // 2
+
+    def x_sent(k, side, h):
+        return k < 2 or h == side
+
+    def x_send(w, k, side, h):
         device = (gx - 1 if side == 0 else gx + 1, gy, gz)
-        if k < 2:
-            return [
-                remote(
-                    w.at[pl.ds(spot_of(plane), FACE), :], hx.at[k, 1 - side],
-                    xs_sem.at[k, side, 0], xr_sem.at[k, 1 - side, 0], device,
-                )
-            ]
-        half = BY // 2
-        return [
+        for n in range(2):
+            plane = n if side == 0 else BX - 2 + n
             remote(
-                w.at[pl.ds(spot_of(plane + n, side * half), half), :],
-                hx.at[k, 1 - side, pl.ds(n * PITCH + side * half, half), :],
-                xs_sem.at[k, side, n], xr_sem.at[k, 1 - side, n], device,
-            )
-            for n in range(2)
-        ]
+                w.at[pl.ds(spot_of(plane, h * half), half), :], hx.at[k, 1 - side, h, n],
+                xs_sem.at[k, side], xr_sem.at[k, 1 - side, h], device,
+            ).start()
+
+    def x_arrived(k, side, h):
+        land = hx.at[k, side, h]
+        remote(land, land, xs_sem.at[k, side], xr_sem.at[k, side, h], partner).wait_recv()
 
     def y_copy(k, side):
         strips = pl.ds(0, BX) if k < 2 else pl.ds(side * (BX // 2), BX // 2)
@@ -220,7 +215,7 @@
         )
 
     def z_copy(k):
-        return remote(zpack.at[k], hz.at[k], zs_sem.at[k], zr_sem.at[k], (gx, gy, 1 - gz))
+        return remote(zpack.at[k], hz.at[k], zs_sem.at[0], zr_sem.at[k], partner)
 
     near_fault = (gy == ny // 2 - 1) | (gy == ny // 2)
     source = gy - (ny // 2 - 1)
@@ -228,31 +223,22 @@
     high_side = jnp.where(gy == ny // 2 - 1, 1.0, 0.0)
     own_rows = BX // ny
 
-    def fault_copy(k, r):
-        owner = lax.rem(gy + r, ny)
-        return remote(
-            trac.at[k, pl.ds(owner * own_rows, own_rows), :], fault.at[source, k],
-            fs_sem.at[k, r - 1], fr_sem.at[source, k], (gx, owner, gz),
-        )
-
-    def send_x(w, k):
-        for side in range(2):
-            @pl.when(has_x[side])
-            def _(side=side):
-                for copy in x_copies(w, k, side):
-                    copy.start()
-
-    def send_fault(k):
+    def send_fault():
         @pl.when(near_fault)
         def _():
             for r in range(1, ny):
-                fault_copy(k, r).start()
-            for i in range(own_rows // 8):
-                fault[source, k, pl.ds(8 * i, 8), :] = trac[
-                    k, pl.ds(pl.multiple_of(gy * own_rows + 8 * i, 8), 8), :
-                ]
-
-    def exchange(w, k):
+                owner = lax.rem(gy + r, ny)
+                remote(
+                    trac.at[:, pl.ds(pl.multiple_of(owner * own_rows, 8), own_rows), :],
+                    fault.at[source], fs_sem.at[0], fr_sem.at[source], (gx, owner, gz),
+                ).start()
+            for k in range(3):
+                for i in range(own_rows // 8):
+                    fault[source, k, pl.ds(8 * i, 8), :] = trac[
+                        k, pl.ds(pl.multiple_of(gy * own_rows + 8 * i, 8), 8), :
+                    ]
+
+    def send_y(w, k):
         for j in range(STRIPS):
             strip = []
             for n, y in enumerate((0, 1, BY - 2, BY - 1)):
@@ -266,13 +252,14 @@
             def _(side=side):
                 y_copy(k, side).start()
 
-        for half in range(BX // SLOTS):
-            def pack(q, acc, half=half):
+    def send_z(w, k):
+        for block in range(BX // SLOTS):
+            def pack(q, acc, block=block):
                 mask = ((lane + 2 - 4 * q) & (BZ - 1)) < 4
                 return tuple(
                     jnp.where(
                         mask,
-                        pltpu.roll(w[pl.ds(spot_of(half * SLOTS + q, 8 * t), 8), :], 4 * q, 1),
+                        pltpu.roll(w[pl.ds(spot_of(block * SLOTS + q, 8 * t), 8), :], 4 * q, 1),
                         acc[t],
                     )
                     for t in range(TILES)
@@ -280,42 +267,42 @@
 
             packed = lax.fori_loop(0, SLOTS, pack, (zero,) * TILES, unroll=2 * UNROLL)
             for t in range(TILES):
-                zpack[k, half * TILES + t] = packed[t]
-
+                zpack[k, block * TILES + t] = packed[t]
         z_copy(k).start()
-        if k == 2:
-            for n in range(3):
-                send_fault(n)
-
-    at_row = lax.rem(lax.broadcasted_iota(jnp.int32, (3 * BZ, BZ), 0), BZ)
-    gap = jnp.abs(at_row - lax.broadcasted_iota(jnp.int32, (3 * BZ, BZ), 1))
-    band[...] = jnp.where(gap == 1, 16.0, jnp.where(gap == 2, -1.0, 0.0)).astype(BF16)
-
-    zero = jnp.zeros((8, BZ), F32)
+
     mu0 = zero
-    for n, i in enumerate(order):
-        first_wait, second_wait = loads[n]
-        first_wait.wait()
-        second_wait.wait()
+    for n, (xa, xb, ya, yb) in enumerate(regions):
+        part = (slice(None), pl.ds(xa, xb - xa), pl.ds(ya, yb - ya))
+        pltpu.make_async_copy(bs.at[part], bs.at[part], in_sem.at[n]).wait()
 
         def start_plane(x, acc):
-            for t in range(TILES):
+            for t in range(ya // 8, yb // 8):
                 at = pl.ds(8 * t, 8)
-                b = bv[x, at, :]
-                inverse = 1.0 / (7.5 + sv[x, at, :])
+                b = bs[0, x, at, :]
+                inverse = 1.0 / (7.5 + bs[1, x, at, :])
                 w = b * inverse
                 w0[pl.ds(spot_of(x, 8 * t), 8), :] = w
                 minv[pl.ds(pl.multiple_of(x * BY, 8) + 8 * t, 8), :] = inverse * (1.0 / 12.0)
                 acc = acc + b * w
             return acc
 
-        mu0 = lax.fori_loop(i * step, (i + 1) * step, start_plane, mu0, unroll=min(step, UNROLL))
+        count = xb - xa
+        tiles = (yb - ya) // 8
+        unroll = max(u for u in range(1, count + 1) if count % u == 0 and u * tiles <= 60 or u == 1)
+        mu0 = lax.fori_loop(xa, xb, start_plane, mu0, unroll=unroll)
         if n == 1:
             pl.semaphore_wait(
                 barrier,
                 1 + one(has_x[0]) + one(has_x[1]) + one(has_y[0]) + one(has_y[1]),
             )
-            send_x(w0, 0)
+            for side in range(2):
+                @pl.when(has_x[side])
+                def _(side=side):
+                    for h in range(2):
+                        x_send(w0, 0, side, h)
+        if n == 3:
+            send_y(w0, 0)
+    send_z(w0, 0)
 
     def edge_terms(d):
         near = jnp.where(place == 1, pltpu.roll(d, BZ - 1, 1), pltpu.roll(d, 1, 1))
@@ -368,7 +355,7 @@
 
         return lax.fori_loop(0, groups // 2, pair, init)
 
-    def fixes(k, apply_x, apply_y):
+    def fixes(k, apply_x, apply_y, then):
         whole = k < 2
         for side in range(2):
             @pl.when(has_y[side])
@@ -384,25 +371,25 @@
                     close = hy[k, side, inner, at, :]
                     apply_y(j, first, 16.0 * close - hy[k, side, outer, at, :])
                     apply_y(j, second, -close)
-        for side in range(2):
-            @pl.when(has_x[side])
-            def _(side=side):
-                for copy in x_copies(w0, k, 1 - side):
-                    copy.wait_recv()
-                inner, outer = (1, 0) if side == 0 else (0, 1)
-                first, second = (0, 1) if side == 0 else (BX - 1, BX - 2)
-                span = range(TILES)
-                if not whole:
-                    span = range((1 - side) * TILES // 2, (2 - side) * TILES // 2)
-                for t in span:
-                    close = hx[k, side, pl.ds(inner * PITCH + 8 * t, 8), :]
-                    distant = hx[k, side, pl.ds(outer * PITCH + 8 * t, 8), :]
-                    apply_x(first, t, 16.0 * close - distant)
-                    apply_x(second, t, -close)
+        for h in range(2):
+            for side in range(2):
+                if not x_sent(k, 1 - side, h):
+                    continue
+
+                @pl.when(has_x[side])
+                def _(side=side, h=h):
+                    x_arrived(k, side, h)
+                    inner, outer = (1, 0) if side == 0 else (0, 1)
+                    first, second = (0, 1) if side == 0 else (BX - 1, BX - 2)
+                    for u in range(TILES // 2):
+                        t = h * (TILES // 2) + u
+                        close = hx[k, side, h, inner, pl.ds(8 * u, 8), :]
+                        distant = hx[k, side, h, outer, pl.ds(8 * u, 8), :]
+                        apply_x(first, t, 16.0 * close - distant)
+                        apply_x(second, t, -close)
+                    then(side, h)
 
     def basis_step(w, new, k, moments, init):
-        exchange(w, k)
-
         def out(x, t, c, n, acc):
             new[pl.ds(spot_of(x, 8 * t), 8), :] = (
                 c - minv[pl.ds(pl.multiple_of(x * BY, 8) + 8 * t, 8), :] * n
@@ -419,25 +406,29 @@
             at = pl.ds(spot_of(8 * j, y), 8, stride=PITCH)
             new[at, :] = new[at, :] - minv[pl.ds(8 * j * BY + y, 8, stride=BY), :] * n
 
-        fixes(k, apply_x, apply_y)
+        def then(side, h):
+            if x_sent(k + 1, side, h):
+                x_send(new, k + 1, side, h)
+
+        fixes(k, apply_x, apply_y, then)
+        send_y(new, k + 1)
         if k > 0:
             await_signals(k - 1, 1 << k)
-        send_x(new, k + 1)
         signal(k, 2 << k)
+        send_z(new, k + 1)
         return sums
 
     basis_step(w0, w1, 0, lambda x, t, c, acc: acc, 0)
 
     def first_moments(x, t, c, acc):
         at = pl.ds(8 * t, 8)
-        return (acc[0] + bv[x, at, :] * c, acc[1] + ((7.5 + sv[x, at, :]) * c) * c)
+        return (acc[0] + bs[0, x, at, :] * c, acc[1] + ((7.5 + bs[1, x, at, :]) * c) * c)
 
     mu1, mu2 = basis_step(w1, w2, 1, first_moments, (zero, zero))
-
-    exchange(w2, 2)
+    send_fault()
 
     def last(x, t, c, n, acc):
-        d = (7.5 + sv[x, pl.ds(8 * t, 8), :]) * c
+        d = (7.5 + bs[1, x, pl.ds(8 * t, 8), :]) * c
         return (
             acc[0] + d * w1[pl.ds(spot_of(x, 8 * t), 8), :],
             acc[1] + d * c,
@@ -445,82 +436,85 @@
         )
 
     mu3, mu4, mu5 = bulk(w2, last, 2, (zero, zero, zero), False)
-    part_a[0] = zero
+    cross_sum[...] = zero
 
     def cross_x(x, t, n):
-        part_a[0] = part_a[0] + w2[pl.ds(spot_of(x, 8 * t), 8), :] * n
+        cross_sum[...] = cross_sum[...] + w2[pl.ds(spot_of(x, 8 * t), 8), :] * n
 
     def cross_y(j, y, n):
-        part_a[0] = part_a[0] + w2[pl.ds(spot_of(8 * j, y), 8, stride=PITCH), :] * n
+        cross_sum[...] = cross_sum[...] + w2[pl.ds(spot_of(8 * j, y), 8, stride=PITCH), :] * n
 
     z_copy(2).wait_recv()
     crossing = zero
     for i in range(packs):
         crossing = crossing + zpack[2, i] * edge_terms(jnp.where(halo_here, hz[2, i], 0.0))
-    fixes(2, cross_x, cross_y)
-    mu5 = mu5 - (2.0 * part_a[0] + crossing) * (1.0 / 12.0)
     await_signals(1, 4)
     signal(2, 8)
+    fixes(2, cross_x, cross_y, lambda side, h: None)
+    mu5 = mu5 - (2.0 * cross_sum[...] + crossing) * (1.0 / 12.0)
 
     local = zero
     for j, m in enumerate((mu0, mu1, mu2, mu3, mu4, mu5)):
         local = jnp.where(row == j, jnp.sum(m, axis=0, keepdims=True), local)
-
-    def reduce(value, buf, s, devices):
-        buf[0] = value
-        copies = [
-            remote(buf.at[0], buf.at[r + 1], rs_sem.at[s, r], rr_sem.at[s, r], device)
-            for r, device in enumerate(devices)
-        ]
-        for c in copies:
-            c.start()
-        for c in copies:
-            c.wait_recv()
-        total = value
+    local = jnp.where(lane == row, jnp.sum(local, axis=1, keepdims=True), 0.0)
+    local = jnp.sum(local, axis=0, keepdims=True)
+
+    def reduce(value, low, buf, s, devices):
+        buf[0, pl.ds(0, 1), :] = value
+        buf[0, pl.ds(1, 1), :] = low
+        for r, device in enumerate(devices):
+            remote(buf.at[0], buf.at[r + 1], rs_sem.at[s], rr_sem.at[s], device).start()
+        land = buf.at[pl.ds(1, len(devices))]
+        remote(land, land, rs_sem.at[s], rr_sem.at[s], partner).wait_recv()
+        terms = [(value, low)]
         for r in range(len(devices)):
-            total = total + buf[r + 1]
-        return total, copies
-
-    total, sent_a = reduce(local, part_a, 0, peers)
+            terms.append((buf[r + 1, pl.ds(0, 1), :], buf[r + 1, pl.ds(1, 1), :]))
+        while len(terms) > 1:
+            pairs = []
+            for a, b in zip(terms[::2], terms[1::2]):
+                h, e = two_sum(a[0], b[0])
+                pairs.append((h, e + (a[1] + b[1])))
+            terms = pairs
+        return terms[0]
+
+    total = reduce(local, jnp.zeros((1, BZ), F32), part_a, 0, peers)
     await_signals(2, 8)
-    total, sent_b = reduce(total, part_b, 1, cross)
+    total = reduce(total[0], total[1], part_b, 1, cross)
 
     mu = []
     for j in range(6):
-        mu.append(lane_sum(jnp.broadcast_to(total[j : j + 1, :], (8, BZ))))
+        mu.append(norm(*(jnp.broadcast_to(v[:, j : j + 1], (8, BZ)) for v in total)))
     for j, c in enumerate(coefficients(mu)):
-        coef[j] = jnp.broadcast_to(c, (8, BZ))
-
-    for k in range(3):
-        for s in range(2):
-            @pl.when(gy != ny // 2 - 1 + s)
-            def _(k=k, s=s):
-                remote(
-                    trac.at[k, pl.ds(0, own_rows), :], fault.at[s, k],
-                    fs_sem.at[k, 0], fr_sem.at[s, k], (gx, gy, 1 - gz),
-                ).wait_recv()
+        coef[j] = c
+
+    for s in range(2):
+        @pl.when(gy != ny // 2 - 1 + s)
+        def _(s=s):
+            land = fault.at[s]
+            remote(land, land, fs_sem.at[0], fr_sem.at[s], partner).wait_recv()
     for k in range(3):
         for i in range(own_rows // 8):
             at = pl.ds(8 * i, 8)
             fault_sum[k, at, :] = fault[0, k, at, :] + fault[1, k, at, :]
 
-    for c in sent_a + sent_b:
-        c.wait_send()
+    for s, buf in enumerate((part_a, part_b)):
+        sent = buf.at[pl.ds(1, buf.shape[0] - 1)]
+        remote(sent, sent, rs_sem.at[s], rr_sem.at[s], partner).wait_send()
+    remote(zpack, hz, zs_sem.at[0], zr_sem.at[0], partner).wait_send()
     for k in range(3):
         for side in range(2):
             @pl.when(has_x[side])
             def _(k=k, side=side):
-                for copy in x_copies(w0, k, side):
-                    copy.wait_send()
+                sent = hx.at[k, side] if k < 2 else hx.at[k, side, 0]
+                remote(sent, sent, xs_sem.at[k, side], xr_sem.at[k, side, 0], partner).wait_send()
             @pl.when(has_y[side])
             def _(k=k, side=side):
                 y_copy(k, side).wait_send()
-        z_copy(k).wait_send()
-
-        @pl.when(near_fault)
-        def _(k=k):
-            for r in range(1, ny):
-                fault_copy(k, r).wait_send()
+
+    @pl.when(near_fault)
+    def _():
+        sent = trac.at[:, pl.ds(0, (ny - 1) * own_rows), :]
+        remote(sent, sent, fs_sem.at[0], fr_sem.at[0], partner).wait_send()
 
 
 def combine(w0, w1, w2, coef, fault_sum, prestress, state, normal, u, slip, buf, sem):
@@ -572,26 +566,26 @@
         in_specs=[pl.BlockSpec(memory_space=pltpu.HBM)] * 2,
         out_specs=[vmem] * 5,
         scratch_shapes=[
-            pltpu.VMEM((BX, BY, BZ), F32),
-            pltpu.VMEM((BX, BY, BZ), F32),
+            pltpu.VMEM((2, BX, BY, BZ), F32),
             pltpu.VMEM((BX * BY, BZ), F32),
             pltpu.VMEM((3, 2, 2, BX, BZ), F32),
             pltpu.VMEM((3, packs, 8, BZ), F32),
             pltpu.VMEM((packs, 8, BZ), F32),
             pltpu.VMEM((3, BX, BZ), F32),
-            pltpu.VMEM((3, 2, FACE, BZ), F32),
+            pltpu.VMEM((3, 2, 2, 2, BY // 2, BZ), F32),
             pltpu.VMEM((3, 2, 2, BX, BZ), F32),
             pltpu.VMEM((3, packs, 8, BZ), F32),
             pltpu.VMEM((2, 3, own, BZ), F32),
-            pltpu.VMEM((group, 8, BZ), F32),
-            pltpu.VMEM((nx, 8, BZ), F32),
+            pltpu.VMEM((group, 2, BZ), F32),
+            pltpu.VMEM((nx, 2, BZ), F32),
+            pltpu.VMEM((8, BZ), F32),
             pltpu.VMEM((3 * BZ, BZ), BF16),
             pltpu.VMEM((GROUP * PITCH, BZ), F32),
             pltpu.VMEM((GROUP * PITCH, BZ), F32),
-            DMA((2, CHUNKS)),
-            DMA((3, 2, 2)), DMA((3, 2, 2)), DMA((3, 2)), DMA((3, 2)), DMA((3,)), DMA((3,)),
-            DMA((3, ny - 1)), DMA((2, 3)),
-            DMA((2, nx - 1)), DMA((2, nx - 1)),
+            DMA((4 + INNER,)),
+            DMA((3, 2)), DMA((3, 2, 2)), DMA((3, 2)), DMA((3, 2)), DMA((1,)), DMA((3,)),
+            DMA((1,)), DMA((2,)),
+            DMA((2,)), DMA((2,)),
             pltpu.SemaphoreType.REGULAR((3, 2)),
         ],
         compiler_params=pltpu.CompilerParams(

time: 34.1 us -> 33.2 us (0.974)
  Pallas kernels: 33.3 us -> 32.4 us
    pallas_call x1, Pallas kernels: 31.2 us -> 30.3 us  [per_device(): pl.pallas_call(krylov, out_shape=[pltpu.VMEM(big, F32), pltpu.VMEM(big, F...]
where the time goes in v5:
time: 33.2 us; the launch traced here: 33.1 us
  Pallas kernels  32.4 us (98%)
  between operations  0.69 us (2%)
    pallas_call x1, Pallas kernels, per_device(): pl.pallas_call(krylov, out_shape=[pltpu.VMEM(big, F32), pltpu.VMEM(big, F...  30.3 us
    pallas_call x1, Pallas kernels, per_device(): pl.pallas_call(combine, out_shape=[jax.ShapeDtypeStruct(load.shape, F32),...  2.09 us

profile of v5, /device:TPU:1, one launch (start us, length us, event | category | flops | bytes accessed | tf_op | source)
XLA Modules:
  0.0 33.1 jit_solution(5102522258986900131)
XLA Ops:
  0.6 0.0 copy-start.2
  0.6 0.0 copy-start.1
  0.7 0.0 copy-start
  0.7 30.3 %krylov.1 = (f32[4904,128]{1,0:T(8,128)S(1)}, f32[4904,128]{1,0:T(8,128)S(1)}, f32[4904,128]{1,0:T(8,128)S(1)}, f32[3,8,128]{2,1,0:T(8,128)S(1)}, f32[3,16,128]{2,1,0:T(8,128)S(1)}) custom-call(f32[64,64,128]{2,1,0:T(8,128)} %load.1, f32[64,64,128]{2,1,0:T(8,128)} %stiff.1), custom_call_target="tpu_custom_call" | custom-call | tf_op jit(solution)/shard_map/krylov/pallas_call | solution.py:560
  31.0 0.0 copy-done.2
  31.0 0.0 copy-done.1
  31.0 0.0 copy-done
  31.0 2.1 %combine.1 = (f32[64,64,128]{2,1,0:T(8,128)}, f32[16,128]{1,0:T(8,128)}) custom-call(f32[4904,128]{1,0:T(8,128)S(1)} %get-tuple-element.7.w0, f32[4904,128]{1,0:T(8,128)S(1)} %get-tuple-element.8.w1, f32[4904,128]{1,0:T(8,128)S(1)} %get-tuple-element.9.w2, f32[3,8,128]{2,1,0:T(8,128)S(1)} %get-tuple-element.10.coef, ...), custom_call_target="tpu_custom_call" | custom-call | tf_op jit(solution)/shard_map/combine/pallas_call | solution.py:596
Async XLA Ops:
  0.6 30.4 %copy-start.2 = (f32[16,128]{1,0:T(8,128)S(1)}, f32[16,128]{1,0:T(8,128)}, u32[]{:S(2)}) copy-start(f32[16,128]{1,0:T(8,128)} %normal.1) | copy-start | bytes 24580
  0.6 30.4 %copy-start.1 = (f32[16,128]{1,0:T(8,128)S(1)}, f32[16,128]{1,0:T(8,128)}, u32[]{:S(2)}) copy-start(f32[16,128]{1,0:T(8,128)} %state.1) | copy-start | bytes 24580
  0.7 30.4 %copy-start = (f32[16,128]{1,0:T(8,128)S(1)}, f32[16,128]{1,0:T(8,128)}, u32[]{:S(2)}) copy-start(f32[16,128]{1,0:T(8,128)} %prestress.1) | copy-start | bytes 24580

commit v6 on v5

--- a/solution.py
+++ b/solution.py
@@ -252,23 +252,14 @@
             def _(side=side):
                 y_copy(k, side).start()
 
-    def send_z(w, k):
-        for block in range(BX // SLOTS):
-            def pack(q, acc, block=block):
+    def pack(w, k, i):
+        for t in range(TILES):
+            packed = zero
+            for q in range(SLOTS):
                 mask = ((lane + 2 - 4 * q) & (BZ - 1)) < 4
-                return tuple(
-                    jnp.where(
-                        mask,
-                        pltpu.roll(w[pl.ds(spot_of(block * SLOTS + q, 8 * t), 8), :], 4 * q, 1),
-                        acc[t],
-                    )
-                    for t in range(TILES)
-                )
-
-            packed = lax.fori_loop(0, SLOTS, pack, (zero,) * TILES, unroll=2 * UNROLL)
-            for t in range(TILES):
-                zpack[k, block * TILES + t] = packed[t]
-        z_copy(k).start()
+                tile = w[pl.ds(spot_of(i * SLOTS + q, 8 * t), 8), :]
+                packed = jnp.where(mask, pltpu.roll(tile, 4 * q, 1), packed)
+            zpack[k, i * TILES + t] = packed
 
     mu0 = zero
     for n, (xa, xb, ya, yb) in enumerate(regions):
@@ -302,7 +293,6 @@
                         x_send(w0, 0, side, h)
         if n == 3:
             send_y(w0, 0)
-    send_z(w0, 0)
 
     def edge_terms(d):
         near = jnp.where(place == 1, pltpu.roll(d, BZ - 1, 1), pltpu.roll(d, 1, 1))
@@ -319,14 +309,14 @@
             jnp.concatenate([high, middle, low], axis=1), band[...], preferred_element_type=F32
         )
 
-    def bulk(w, out, k, init, with_halo):
-        if with_halo:
-            z_copy(k).wait_recv()
-            for i in range(packs):
-                edge[i] = edge_terms(jnp.where(halo_here, hz[k, i], 0.0))
-        mask = ((lane + 2) & (BZ - 1)) < 4
-
-        def group(g, zz, acc):
+    edge_mask = ((lane + 2) & (BZ - 1)) < 4
+
+    def z_term(x, t):
+        turn = lax.rem(BZ - 4 * lax.rem(x, SLOTS), BZ)
+        return jnp.where(edge_mask, pltpu.roll(edge[(x // SLOTS) * TILES + t], turn, 1), 0.0)
+
+    def bulk(w, out, k, init, z_fix=None):
+        def group(g, zz, acc, with_z):
             for t in range(TILES):
                 def at(p, dy):
                     return w[pl.ds(spot_of(g * GROUP, 8 * t) + (p * PITCH + dy), 8), :]
@@ -337,23 +327,43 @@
                     near = (line[p + 3] + line[p + 1]) + (at(p, 1) + at(p, -1))
                     far = (line[p + 4] + line[p]) + (at(p, 2) + at(p, -2))
                     n = (16.0 * near - far) + zz[pl.ds(p * PITCH + 8 * t, 8), :]
-                    if with_halo:
-                        turn = lax.rem(BZ - 4 * lax.rem(x, SLOTS), BZ)
-                        e = pltpu.roll(edge[(x // SLOTS) * TILES + t], turn, 1)
-                        n = n + jnp.where(mask, e, 0.0)
+                    if with_z:
+                        n = n + z_term(x, t)
                     acc = out(x, t, line[p + 2], n, acc)
             return acc
 
         groups = BX // GROUP
         even[...] = along_z(w, 0)
 
-        def pair(i, acc):
+        pairs = groups // 2
+        ends = BX // SLOTS
+        inside = (pairs - ends) * 2 * GROUP // ends
+
+        def pair(i, acc, with_z=False):
             odd[...] = along_z(w, (2 * i + 1) * GROUP)
-            acc = group(2 * i, even, acc)
+            acc = group(2 * i, even, acc, with_z)
             even[...] = along_z(w, jnp.minimum(2 * i + 2, groups - 1) * GROUP)
-            return group(2 * i + 1, odd, acc)
-
-        return lax.fori_loop(0, groups // 2, pair, init)
+            return group(2 * i + 1, odd, acc, with_z)
+
+        def first_pair(i, acc):
+            pack(w, k, i)
+            return pair(i, acc)
+
+        def last_pair(i, acc):
+            for p in range(inside):
+                for t in range(TILES):
+                    z_fix((i - (pairs - ends)) * inside + p, t)
+            return pair(i, acc, True)
+
+        acc = lax.fori_loop(0, ends, first_pair, init)
+        z_copy(k).start()
+        if z_fix is None:
+            return lax.fori_loop(ends, pairs, pair, acc)
+        acc = lax.fori_loop(ends, pairs - ends, pair, acc)
+        z_copy(k).wait_recv()
+        for i in range(packs):
+            edge[i] = edge_terms(jnp.where(halo_here, hz[k, i], 0.0))
+        return lax.fori_loop(pairs - ends, pairs, last_pair, acc)
 
     def fixes(k, apply_x, apply_y, then):
         whole = k < 2
@@ -396,7 +406,12 @@
             )
             return moments(x, t, c, acc)
 
-        sums = bulk(w, out, k, init, True)
+        def z_fix(x, t):
+            at = pl.ds(spot_of(x, 8 * t), 8)
+            m = minv[pl.ds(pl.multiple_of(x * BY, 8) + 8 * t, 8), :]
+            new[at, :] = new[at, :] - m * z_term(x, t)
+
+        sums = bulk(w, out, k, init, z_fix)
 
         def apply_x(x, t, n):
             at = pl.ds(spot_of(x, 8 * t), 8)
@@ -415,7 +430,6 @@
         if k > 0:
             await_signals(k - 1, 1 << k)
         signal(k, 2 << k)
-        send_z(new, k + 1)
         return sums
 
     basis_step(w0, w1, 0, lambda x, t, c, acc: acc, 0)
@@ -435,7 +449,7 @@
             acc[2] + c * (d - n * (1.0 / 12.0)),
         )
 
-    mu3, mu4, mu5 = bulk(w2, last, 2, (zero, zero, zero), False)
+    mu3, mu4, mu5 = bulk(w2, last, 2, (zero, zero, zero))
     cross_sum[...] = zero
 
     def cross_x(x, t, n):

time: 33.2 us -> 31.3 us (0.943)
  Pallas kernels: 32.4 us -> 30.5 us
    pallas_call x1, Pallas kernels: 30.3 us -> 28.4 us  [per_device(): pl.pallas_call(krylov, out_shape=[pltpu.VMEM(big, F32), pltpu.VMEM(big, F...]
where the time goes in v6:
time: 31.3 us; the launch traced here: 31.2 us
  Pallas kernels  30.5 us (97%)
  between operations  0.69 us (2%)
    pallas_call x1, Pallas kernels, per_device(): pl.pallas_call(krylov, out_shape=[pltpu.VMEM(big, F32), pltpu.VMEM(big, F...  28.4 us
    pallas_call x1, Pallas kernels, per_device(): pl.pallas_call(combine, out_shape=[jax.ShapeDtypeStruct(load.shape, F32),...  2.09 us

profile of v6, /device:TPU:1, one launch (start us, length us, event | category | flops | bytes accessed | tf_op | source)
XLA Modules:
  0.0 31.2 jit_solution(14650476041820650136)
XLA Ops:
  0.6 0.0 copy-start.2
  0.6 0.0 copy-start.1
  0.7 0.0 copy-start
  0.7 28.4 %krylov.1 = (f32[4904,128]{1,0:T(8,128)S(1)}, f32[4904,128]{1,0:T(8,128)S(1)}, f32[4904,128]{1,0:T(8,128)S(1)}, f32[3,8,128]{2,1,0:T(8,128)S(1)}, f32[3,16,128]{2,1,0:T(8,128)S(1)}) custom-call(f32[64,64,128]{2,1,0:T(8,128)} %load.1, f32[64,64,128]{2,1,0:T(8,128)} %stiff.1), custom_call_target="tpu_custom_call" | custom-call | tf_op jit(solution)/shard_map/krylov/pallas_call | solution.py:574
  29.1 0.0 copy-done.2
  29.1 0.0 copy-done.1
  29.1 0.0 copy-done
  29.1 2.1 %combine.1 = (f32[64,64,128]{2,1,0:T(8,128)}, f32[16,128]{1,0:T(8,128)}) custom-call(f32[4904,128]{1,0:T(8,128)S(1)} %get-tuple-element.7.w0, f32[4904,128]{1,0:T(8,128)S(1)} %get-tuple-element.8.w1, f32[4904,128]{1,0:T(8,128)S(1)} %get-tuple-element.9.w2, f32[3,8,128]{2,1,0:T(8,128)S(1)} %get-tuple-element.10.coef, ...), custom_call_target="tpu_custom_call" | custom-call | tf_op jit(solution)/shard_map/combine/pallas_call | solution.py:610
Async XLA Ops:
  0.6 28.4 %copy-start.2 = (f32[16,128]{1,0:T(8,128)S(1)}, f32[16,128]{1,0:T(8,128)}, u32[]{:S(2)}) copy-start(f32[16,128]{1,0:T(8,128)} %normal.1) | copy-start | bytes 24580
  0.6 28.4 %copy-start.1 = (f32[16,128]{1,0:T(8,128)S(1)}, f32[16,128]{1,0:T(8,128)}, u32[]{:S(2)}) copy-start(f32[16,128]{1,0:T(8,128)} %state.1) | copy-start | bytes 24580
  0.7 28.4 %copy-start = (f32[16,128]{1,0:T(8,128)S(1)}, f32[16,128]{1,0:T(8,128)}, u32[]{:S(2)}) copy-start(f32[16,128]{1,0:T(8,128)} %prestress.1) | copy-start | bytes 24580

commit v7 on v6

--- a/solution.py
+++ b/solution.py
@@ -109,13 +109,11 @@
 def krylov(
     load, stiff, w0, w1, w2, coef, fault_sum,
     bs, minv, ypack, zpack, edge, trac,
-    hx, hy, hz, fault, part_a, part_b, cross_sum, band, even, odd,
-    in_sem, xs_sem, xr_sem, ys_sem, yr_sem, zs_sem, zr_sem, fs_sem, fr_sem, rs_sem, rr_sem, token,
+    hx, hy, hz, fault, part_a, cross_sum, band, even, odd,
+    in_sem, xs_sem, xr_sem, ys_sem, yr_sem, zs_sem, zr_sem, fs_sem, fr_sem, rs_sem, rr_sem, token, column,
 ):
     gx, gy, gz = (lax.axis_index(a) for a in ("gx", "gy", "gz"))
     nx, ny, nz = (lax.axis_size(a) for a in ("gx", "gy", "gz"))
-    group = ny * nz
-    spot = gy * nz + gz
     lane = lax.broadcasted_iota(jnp.int32, (8, BZ), 1)
     row = lax.broadcasted_iota(jnp.int32, (8, BZ), 0)
     place = (lane + 2) & 3
@@ -134,11 +132,25 @@
             pltpu.make_async_copy(source.at[part], bs.at[(i,) + part], in_sem.at[n]).start()
 
     barrier = pltpu.get_barrier_semaphore()
-    peers = []
-    for r in range(1, group):
-        other = lax.rem(spot + r, group)
-        peers.append((gx, other // nz, lax.rem(other, nz)))
-    cross = [(lax.rem(gx + r, nx), gy, gz) for r in range(1, nx)]
+    side_x = 4 if nx % 4 == 0 else nx
+    offsets = [
+        (dy, dx, dz, dc)
+        for dy in range(nx // side_x) for dx in range(side_x) for dz in range(ny) for dc in range(nz)
+    ]
+
+    def hops(o):
+        sizes = (nx // side_x, side_x, ny)
+        return sum(min(d, n - d) for d, n in zip(o, sizes)) + 0.5 * o[3]
+
+    offsets = sorted(offsets, key=hops, reverse=True)[:-1]
+    everyone = [
+        (
+            lax.rem(gx // side_x + dy, nx // side_x) * side_x + lax.rem(gx + dx, side_x),
+            lax.rem(gy + dz, ny),
+            lax.rem(gz + dc, nz),
+        )
+        for dy, dx, dz, dc in offsets
+    ]
     has_x = (gx > 0, gx < nx - 1)
     has_y = (gy > 0, gy < ny - 1)
 
@@ -357,10 +369,19 @@
 
         acc = lax.fori_loop(0, ends, first_pair, init)
         z_copy(k).start()
-        if z_fix is None:
-            return lax.fori_loop(ends, pairs, pair, acc)
         acc = lax.fori_loop(ends, pairs - ends, pair, acc)
         z_copy(k).wait_recv()
+        if k == 2:
+            await_signals(2, 8)
+            for r in range(1, ny):
+                pl.semaphore_signal(
+                    column.at[0], inc=1, device_id=(gx, lax.rem(gy + r, ny), gz),
+                    device_id_type=MESH,
+                )
+            return lax.fori_loop(pairs - ends, pairs, pair, acc)
+        if k == 1:
+            await_signals(0, 2)
+            signal(1, 4)
         for i in range(packs):
             edge[i] = edge_terms(jnp.where(halo_here, hz[k, i], 0.0))
         return lax.fori_loop(pairs - ends, pairs, last_pair, acc)
@@ -427,9 +448,11 @@
 
         fixes(k, apply_x, apply_y, then)
         send_y(new, k + 1)
-        if k > 0:
-            await_signals(k - 1, 1 << k)
-        signal(k, 2 << k)
+        if k == 0:
+            signal(0, 2)
+        else:
+            await_signals(1, 4)
+            signal(2, 8)
         return sums
 
     basis_step(w0, w1, 0, lambda x, t, c, acc: acc, 0)
@@ -458,12 +481,9 @@
     def cross_y(j, y, n):
         cross_sum[...] = cross_sum[...] + w2[pl.ds(spot_of(8 * j, y), 8, stride=PITCH), :] * n
 
-    z_copy(2).wait_recv()
     crossing = zero
     for i in range(packs):
         crossing = crossing + zpack[2, i] * edge_terms(jnp.where(halo_here, hz[2, i], 0.0))
-    await_signals(1, 4)
-    signal(2, 8)
     fixes(2, cross_x, cross_y, lambda side, h: None)
     mu5 = mu5 - (2.0 * cross_sum[...] + crossing) * (1.0 / 12.0)
 
@@ -473,16 +493,15 @@
     local = jnp.where(lane == row, jnp.sum(local, axis=1, keepdims=True), 0.0)
     local = jnp.sum(local, axis=0, keepdims=True)
 
-    def reduce(value, low, buf, s, devices):
-        buf[0, pl.ds(0, 1), :] = value
-        buf[0, pl.ds(1, 1), :] = low
-        for r, device in enumerate(devices):
-            remote(buf.at[0], buf.at[r + 1], rs_sem.at[s], rr_sem.at[s], device).start()
-        land = buf.at[pl.ds(1, len(devices))]
-        remote(land, land, rs_sem.at[s], rr_sem.at[s], partner).wait_recv()
-        terms = [(value, low)]
-        for r in range(len(devices)):
-            terms.append((buf[r + 1, pl.ds(0, 1), :], buf[r + 1, pl.ds(1, 1), :]))
+    pl.semaphore_wait(column.at[0], ny - 1)
+    last_slot = len(everyone)
+    part_a[last_slot] = local
+    for r, device in enumerate(everyone):
+        remote(part_a.at[last_slot], part_a.at[r], rs_sem.at[0], rr_sem.at[0], device).start()
+    land = part_a.at[pl.ds(0, last_slot)]
+    remote(land, land, rs_sem.at[0], rr_sem.at[0], partner).wait_recv()
+
+    def tree(terms):
         while len(terms) > 1:
             pairs = []
             for a, b in zip(terms[::2], terms[1::2]):
@@ -491,9 +510,11 @@
             terms = pairs
         return terms[0]
 
-    total = reduce(local, jnp.zeros((1, BZ), F32), part_a, 0, peers)
-    await_signals(2, 8)
-    total = reduce(total[0], total[1], part_b, 1, cross)
+    rows = [
+        (part_a[pl.ds(8 * i, 8)].reshape(8, BZ), zero) for i in range((last_slot + 1) // 8)
+    ]
+    high, low = tree(rows)
+    total = tree([(high[i : i + 1], low[i : i + 1]) for i in range(8)])
 
     mu = []
     for j in range(6):
@@ -511,9 +532,7 @@
             at = pl.ds(8 * i, 8)
             fault_sum[k, at, :] = fault[0, k, at, :] + fault[1, k, at, :]
 
-    for s, buf in enumerate((part_a, part_b)):
-        sent = buf.at[pl.ds(1, buf.shape[0] - 1)]
-        remote(sent, sent, rs_sem.at[s], rr_sem.at[s], partner).wait_send()
+    remote(land, land, rs_sem.at[0], rr_sem.at[0], partner).wait_send()
     remote(zpack, hz, zs_sem.at[0], zr_sem.at[0], partner).wait_send()
     for k in range(3):
         for side in range(2):
@@ -590,8 +609,7 @@
             pltpu.VMEM((3, 2, 2, BX, BZ), F32),
             pltpu.VMEM((3, packs, 8, BZ), F32),
             pltpu.VMEM((2, 3, own, BZ), F32),
-            pltpu.VMEM((group, 2, BZ), F32),
-            pltpu.VMEM((nx, 2, BZ), F32),
+            pltpu.VMEM((group * nx, 1, BZ), F32),
             pltpu.VMEM((8, BZ), F32),
             pltpu.VMEM((3 * BZ, BZ), BF16),
             pltpu.VMEM((GROUP * PITCH, BZ), F32),
@@ -599,8 +617,9 @@
             DMA((4 + INNER,)),
             DMA((3, 2)), DMA((3, 2, 2)), DMA((3, 2)), DMA((3, 2)), DMA((1,)), DMA((3,)),
             DMA((1,)), DMA((2,)),
-            DMA((2,)), DMA((2,)),
+            DMA((1,)), DMA((1,)),
             pltpu.SemaphoreType.REGULAR((3, 2)),
+            pltpu.SemaphoreType.REGULAR((1,)),
         ],
         compiler_params=pltpu.CompilerParams(
             collective_id=0, has_side_effects=True, vmem_limit_bytes=55 * 2**20

time: 31.3 us -> 29.9 us (0.955)
  Pallas kernels: 30.5 us -> 29.1 us
    pallas_call x1, Pallas kernels: 28.4 us -> 27 us  [per_device(): pl.pallas_call(krylov, out_shape=[pltpu.VMEM(big, F32), pltpu.VMEM(big, F...]
where the time goes in v7:
time: 29.9 us; the launch traced here: 29.8 us
  Pallas kernels  29.1 us (97%)
  between operations  0.69 us (2%)
    pallas_call x1, Pallas kernels, per_device(): pl.pallas_call(krylov, out_shape=[pltpu.VMEM(big, F32), pltpu.VMEM(big, F...  27 us
    pallas_call x1, Pallas kernels, per_device(): pl.pallas_call(combine, out_shape=[jax.ShapeDtypeStruct(load.shape, F32),...  2.09 us

profile of v7, /device:TPU:1, one launch (start us, length us, event | category | flops | bytes accessed | tf_op | source)
XLA Modules:
  0.0 29.8 jit_solution(3657192477868692652)
XLA Ops:
  0.6 0.0 copy-start.2
  0.6 0.0 copy-start.1
  0.7 0.0 copy-start
  0.7 27.0 %krylov.1 = (f32[4904,128]{1,0:T(8,128)S(1)}, f32[4904,128]{1,0:T(8,128)S(1)}, f32[4904,128]{1,0:T(8,128)S(1)}, f32[3,8,128]{2,1,0:T(8,128)S(1)}, f32[3,16,128]{2,1,0:T(8,128)S(1)}) custom-call(f32[64,64,128]{2,1,0:T(8,128)} %load.1, f32[64,64,128]{2,1,0:T(8,128)} %stiff.1), custom_call_target="tpu_custom_call" | custom-call | tf_op jit(solution)/shard_map/krylov/pallas_call | solution.py:593
  27.7 0.0 copy-done.2
  27.7 0.0 copy-done.1
  27.7 0.0 copy-done
  27.7 2.1 %combine.1 = (f32[64,64,128]{2,1,0:T(8,128)}, f32[16,128]{1,0:T(8,128)}) custom-call(f32[4904,128]{1,0:T(8,128)S(1)} %get-tuple-element.7.w0, f32[4904,128]{1,0:T(8,128)S(1)} %get-tuple-element.8.w1, f32[4904,128]{1,0:T(8,128)S(1)} %get-tuple-element.9.w2, f32[3,8,128]{2,1,0:T(8,128)S(1)} %get-tuple-element.10.coef, ...), custom_call_target="tpu_custom_call" | custom-call | tf_op jit(solution)/shard_map/combine/pallas_call | solution.py:629
Async XLA Ops:
  0.6 27.0 %copy-start.2 = (f32[16,128]{1,0:T(8,128)S(1)}, f32[16,128]{1,0:T(8,128)}, u32[]{:S(2)}) copy-start(f32[16,128]{1,0:T(8,128)} %normal.1) | copy-start | bytes 24580
  0.6 27.0 %copy-start.1 = (f32[16,128]{1,0:T(8,128)S(1)}, f32[16,128]{1,0:T(8,128)}, u32[]{:S(2)}) copy-start(f32[16,128]{1,0:T(8,128)} %state.1) | copy-start | bytes 24580
  0.7 27.0 %copy-start = (f32[16,128]{1,0:T(8,128)S(1)}, f32[16,128]{1,0:T(8,128)}, u32[]{:S(2)}) copy-start(f32[16,128]{1,0:T(8,128)} %prestress.1) | copy-start | bytes 24580

commit v8 on v7

--- a/solution.py
+++ b/solution.py
@@ -110,7 +110,7 @@
     load, stiff, w0, w1, w2, coef, fault_sum,
     bs, minv, ypack, zpack, edge, trac,
     hx, hy, hz, fault, part_a, cross_sum, band, even, odd,
-    in_sem, xs_sem, xr_sem, ys_sem, yr_sem, zs_sem, zr_sem, fs_sem, fr_sem, rs_sem, rr_sem, token, column,
+    in_sem, xs_sem, xr_sem, ys_sem, yr_sem, zs_sem, zr_sem, fs_sem, fr_sem, rs_sem, rr_sem, token,
 ):
     gx, gy, gz = (lax.axis_index(a) for a in ("gx", "gy", "gz"))
     nx, ny, nz = (lax.axis_size(a) for a in ("gx", "gy", "gz"))
@@ -157,34 +157,34 @@
     def one(flag):
         return jnp.where(flag, 1, 0)
 
-    def sides(distance):
-        return ((gx >= distance, gx - distance), (gx + distance < nx, gx + distance))
-
-    def signal(k, distance):
-        for side, (there, target) in enumerate(sides(distance)):
+    def reach(distances):
+        return [
+            pair
+            for n in distances
+            for pair in ((gx >= n, gx - n), (gx + n < nx, gx + n))
+        ]
+
+    def tell(sem, distances):
+        for there, target in reach(distances):
             @pl.when(there)
-            def _(side=side, target=target):
-                pl.semaphore_signal(
-                    token.at[k, 1 - side], inc=1, device_id=(target, gy, gz), device_id_type=MESH
-                )
-
-    def await_signals(k, distance):
-        for side, (there, _) in enumerate(sides(distance)):
-            @pl.when(there)
-            def _(side=side):
-                pl.semaphore_wait(token.at[k, side], 1)
-
-    for there, target in sides(1):
-        @pl.when(there)
-        def _(target=target):
-            pl.semaphore_signal(barrier, inc=1, device_id=(target, gy, gz), device_id_type=MESH)
-    for side in range(2):
-        @pl.when(has_y[side])
-        def _(side=side):
-            pl.semaphore_signal(
-                barrier, inc=1, device_id=(gx, gy + 2 * side - 1, gz), device_id_type=MESH
-            )
-    pl.semaphore_signal(barrier, inc=1, device_id=(gx, gy, 1 - gz), device_id_type=MESH)
+            def _(target=target):
+                pl.semaphore_signal(sem, inc=1, device_id=(target, gy, gz), device_id_type=MESH)
+
+    def hear(sem, distances):
+        count = sum(one(there) for there, _ in reach(distances))
+
+        @pl.when(count > 0)
+        def _():
+            pl.semaphore_wait(sem, count)
+
+    near, far = (1, 2, 3), (4, 8, 12)
+    tell(barrier, near + far)
+    column = [
+        (gx, lax.rem(gy + dz, ny), lax.rem(gz + dc, nz))
+        for dz in range(ny) for dc in range(nz) if dz or dc
+    ]
+    for device in column:
+        pl.semaphore_signal(barrier, inc=1, device_id=device, device_id_type=MESH)
 
     for w in (w0, w1, w2):
         zero_edges(w)
@@ -295,14 +295,14 @@
         mu0 = lax.fori_loop(xa, xb, start_plane, mu0, unroll=unroll)
         if n == 1:
             pl.semaphore_wait(
-                barrier,
-                1 + one(has_x[0]) + one(has_x[1]) + one(has_y[0]) + one(has_y[1]),
+                barrier, len(column) + sum(one(there) for there, _ in reach(near + far))
             )
             for side in range(2):
                 @pl.when(has_x[side])
                 def _(side=side):
                     for h in range(2):
                         x_send(w0, 0, side, h)
+            tell(token.at[0], near)
         if n == 3:
             send_y(w0, 0)
 
@@ -372,16 +372,10 @@
         acc = lax.fori_loop(ends, pairs - ends, pair, acc)
         z_copy(k).wait_recv()
         if k == 2:
-            await_signals(2, 8)
-            for r in range(1, ny):
-                pl.semaphore_signal(
-                    column.at[0], inc=1, device_id=(gx, lax.rem(gy + r, ny), gz),
-                    device_id_type=MESH,
-                )
             return lax.fori_loop(pairs - ends, pairs, pair, acc)
-        if k == 1:
-            await_signals(0, 2)
-            signal(1, 4)
+        hear(token.at[k], near if k == 0 else far)
+        if k == 0:
+            tell(token.at[1], far)
         for i in range(packs):
             edge[i] = edge_terms(jnp.where(halo_here, hz[k, i], 0.0))
         return lax.fori_loop(pairs - ends, pairs, last_pair, acc)
@@ -448,11 +442,6 @@
 
         fixes(k, apply_x, apply_y, then)
         send_y(new, k + 1)
-        if k == 0:
-            signal(0, 2)
-        else:
-            await_signals(1, 4)
-            signal(2, 8)
         return sums
 
     basis_step(w0, w1, 0, lambda x, t, c, acc: acc, 0)
@@ -493,7 +482,6 @@
     local = jnp.where(lane == row, jnp.sum(local, axis=1, keepdims=True), 0.0)
     local = jnp.sum(local, axis=0, keepdims=True)
 
-    pl.semaphore_wait(column.at[0], ny - 1)
     last_slot = len(everyone)
     part_a[last_slot] = local
     for r, device in enumerate(everyone):
@@ -618,8 +606,7 @@
             DMA((3, 2)), DMA((3, 2, 2)), DMA((3, 2)), DMA((3, 2)), DMA((1,)), DMA((3,)),
             DMA((1,)), DMA((2,)),
             DMA((1,)), DMA((1,)),
-            pltpu.SemaphoreType.REGULAR((3, 2)),
-            pltpu.SemaphoreType.REGULAR((1,)),
+            pltpu.SemaphoreType.REGULAR((2,)),
         ],
         compiler_params=pltpu.CompilerParams(
             collective_id=0, has_side_effects=True, vmem_limit_bytes=55 * 2**20

time: 29.9 us -> 29.7 us (level)
  no operation moved by 1% of the time
where the time goes in v8:
time: 29.7 us; the launch traced here: 29.6 us
  Pallas kernels  28.9 us (97%)
  between operations  0.69 us (2%)
    pallas_call x1, Pallas kernels, per_device(): pl.pallas_call(krylov, out_shape=[pltpu.VMEM(big, F32), pltpu.VMEM(big, F...  26.8 us
    pallas_call x1, Pallas kernels, per_device(): pl.pallas_call(combine, out_shape=[jax.ShapeDtypeStruct(load.shape, F32),...  2.09 us

profile of v8, /device:TPU:1, one launch (start us, length us, event | category | flops | bytes accessed | tf_op | source)
XLA Modules:
  0.0 29.6 jit_solution(11251950568111313538)
XLA Ops:
  0.6 0.0 copy-start.2
  0.6 0.0 copy-start.1
  0.7 0.0 copy-start
  0.7 26.8 %krylov.1 = (f32[4904,128]{1,0:T(8,128)S(1)}, f32[4904,128]{1,0:T(8,128)S(1)}, f32[4904,128]{1,0:T(8,128)S(1)}, f32[3,8,128]{2,1,0:T(8,128)S(1)}, f32[3,16,128]{2,1,0:T(8,128)S(1)}) custom-call(f32[64,64,128]{2,1,0:T(8,128)} %load.1, f32[64,64,128]{2,1,0:T(8,128)} %stiff.1), custom_call_target="tpu_custom_call" | custom-call | tf_op jit(solution)/shard_map/krylov/pallas_call | solution.py:581
  27.5 0.0 copy-done.2
  27.5 0.0 copy-done.1
  27.5 0.0 copy-done
  27.5 2.1 %combine.1 = (f32[64,64,128]{2,1,0:T(8,128)}, f32[16,128]{1,0:T(8,128)}) custom-call(f32[4904,128]{1,0:T(8,128)S(1)} %get-tuple-element.7.w0, f32[4904,128]{1,0:T(8,128)S(1)} %get-tuple-element.8.w1, f32[4904,128]{1,0:T(8,128)S(1)} %get-tuple-element.9.w2, f32[3,8,128]{2,1,0:T(8,128)S(1)} %get-tuple-element.10.coef, ...), custom_call_target="tpu_custom_call" | custom-call | tf_op jit(solution)/shard_map/combine/pallas_call | solution.py:616
Async XLA Ops:
  0.6 26.8 %copy-start.2 = (f32[16,128]{1,0:T(8,128)S(1)}, f32[16,128]{1,0:T(8,128)}, u32[]{:S(2)}) copy-start(f32[16,128]{1,0:T(8,128)} %normal.1) | copy-start | bytes 24580
  0.6 26.8 %copy-start.1 = (f32[16,128]{1,0:T(8,128)S(1)}, f32[16,128]{1,0:T(8,128)}, u32[]{:S(2)}) copy-start(f32[16,128]{1,0:T(8,128)} %state.1) | copy-start | bytes 24580
  0.7 26.8 %copy-start = (f32[16,128]{1,0:T(8,128)S(1)}, f32[16,128]{1,0:T(8,128)}, u32[]{:S(2)}) copy-start(f32[16,128]{1,0:T(8,128)} %prestress.1) | copy-start | bytes 24580

commit v9 on v8

--- a/solution.py
+++ b/solution.py
@@ -17,7 +17,7 @@
 TILES = BY // 8
 STRIPS = BX // 8
 CHUNKS = 8
-INNER = 6
+INNER = 3
 SLOTS = 32
 GROUP = 4
 UNROLL = 8

time: 29.7 us -> 29.6 us (level)
  no operation moved by 1% of the time
where the time goes in v9:
time: 29.6 us; the launch traced here: 29.5 us
  Pallas kernels  28.8 us (97%)
  between operations  0.69 us (2%)
    pallas_call x1, Pallas kernels, per_device(): pl.pallas_call(krylov, out_shape=[pltpu.VMEM(big, F32), pltpu.VMEM(big, F...  26.8 us
    pallas_call x1, Pallas kernels, per_device(): pl.pallas_call(combine, out_shape=[jax.ShapeDtypeStruct(load.shape, F32),...  2.09 us

profile of v9, /device:TPU:1, one launch (start us, length us, event | category | flops | bytes accessed | tf_op | source)
XLA Modules:
  0.0 29.5 jit_solution(6773424707882551476)
XLA Ops:
  0.6 0.0 copy-start.2
  0.6 0.0 copy-start.1
  0.7 0.0 copy-start
  0.7 26.8 %krylov.1 = (f32[4904,128]{1,0:T(8,128)S(1)}, f32[4904,128]{1,0:T(8,128)S(1)}, f32[4904,128]{1,0:T(8,128)S(1)}, f32[3,8,128]{2,1,0:T(8,128)S(1)}, f32[3,16,128]{2,1,0:T(8,128)S(1)}) custom-call(f32[64,64,128]{2,1,0:T(8,128)} %load.1, f32[64,64,128]{2,1,0:T(8,128)} %stiff.1), custom_call_target="tpu_custom_call" | custom-call | tf_op jit(solution)/shard_map/krylov/pallas_call | solution.py:581
  27.4 0.0 copy-done.2
  27.4 0.0 copy-done.1
  27.4 0.0 copy-done
  27.5 2.1 %combine.1 = (f32[64,64,128]{2,1,0:T(8,128)}, f32[16,128]{1,0:T(8,128)}) custom-call(f32[4904,128]{1,0:T(8,128)S(1)} %get-tuple-element.7.w0, f32[4904,128]{1,0:T(8,128)S(1)} %get-tuple-element.8.w1, f32[4904,128]{1,0:T(8,128)S(1)} %get-tuple-element.9.w2, f32[3,8,128]{2,1,0:T(8,128)S(1)} %get-tuple-element.10.coef, ...), custom_call_target="tpu_custom_call" | custom-call | tf_op jit(solution)/shard_map/combine/pallas_call | solution.py:616
Async XLA Ops:
  0.6 26.8 %copy-start.2 = (f32[16,128]{1,0:T(8,128)S(1)}, f32[16,128]{1,0:T(8,128)}, u32[]{:S(2)}) copy-start(f32[16,128]{1,0:T(8,128)} %normal.1) | copy-start | bytes 24580
  0.6 26.8 %copy-start.1 = (f32[16,128]{1,0:T(8,128)S(1)}, f32[16,128]{1,0:T(8,128)}, u32[]{:S(2)}) copy-start(f32[16,128]{1,0:T(8,128)} %state.1) | copy-start | bytes 24580
  0.7 26.8 %copy-start = (f32[16,128]{1,0:T(8,128)S(1)}, f32[16,128]{1,0:T(8,128)}, u32[]{:S(2)}) copy-start(f32[16,128]{1,0:T(8,128)} %prestress.1) | copy-start | bytes 24580
